TPU v7x, 32 devices: a whole 2x2x4 slice. The times are simulated.
32 devices in a mesh: tile: 8 (over z, x), lev: 4 (over y, core).
Axes of the slice: x: 2, y: 2, z: 4, core: 2. Of those that a mesh axis runs over, the one named last changes fastest.
Arguments:
- mixing: float32 [3, 64, 32768], P(None, 'lev', 'tile'), may hold values from 0.05 to 3
- density: float32 [64, 32768], P('lev', 'tile'), may hold values from 0.4 to 1.2
- routes: int32 [32768, 1], P('tile'), may hold values from 0 to 7; in each aligned block of 4096 rows (0 to 4095, 4096 to 8191, ...) at most 1024 rows name the same one
- beam_weight: float32 [8, 168, 64], P('tile'), may hold values from 0.001 to 0.06
- gate_adjoint: float32 [168, 65536], P('lev', 'tile'), may hold values from -6 to 6
Outputs:
- gate_values: float32 [168, 65536], P('lev', 'tile')
- increments: float32 [3, 64, 32768], P(None, 'lev', 'tile')
Inputs may be any that keep to these rules, and one draw needn't show every extreme that they name: `routes`: each column names the site that observes it; the columns of one tile index send at most 1024 columns to one site, and exactly 1024 to some site.
All inputs are finite; a program needn't handle non-finite values.
Results may differ from a plain program's by a relative error of at most 0.00007.
Values sent between devices are 32-bit elements; how exact they have to be, the bound alone decides.
No kernel may reach another device: no remote copies, remote signals or barrier semaphores. Data moves between devices by JAX's collectives and lax.ppermute only.
A program may use at most 64 MiB of HBM per device.

v0:
```python
import functools

import jax
import jax.numpy as jnp
from jax import lax
from jax.experimental import pallas as pl
from jax.experimental.pallas import tpu as pltpu
from jax.sharding import PartitionSpec as P

coefficients = (3.63, 0.96, 1.98)
exponents = (1.75, 1.66, 1.75)
LANES = 128
ROWS = 8
GROUP = 8
DIRECT = 8
SMEM = pltpu.SMEM


def iota(shape, dim):
    return lax.broadcasted_iota(jnp.int32, shape, dim)


def tile_at(index):
    return pl.ds(pl.multiple_of(index * LANES, LANES), LANES)


def halves(x):
    high = x.astype(jnp.bfloat16)
    low = (x - high.astype(jnp.float32)).astype(jnp.bfloat16)
    return high, low


def split_dot(weights, x):
    w_high, w_low = halves(weights)
    x_high, x_low = halves(x)
    rows = weights.shape[0]
    both = jnp.dot(jnp.concatenate([w_high, w_low], 0), x_high, preferred_element_type=jnp.float32)
    rest = jnp.dot(w_high, x_low, preferred_element_type=jnp.float32)
    return both[:rows] + (both[rows:] + rest)


def first_target(targets):
    return lax.axis_index("tile") if targets <= DIRECT else 0


def blocks_of(refs):
    return [ref.at[i] for ref in refs if len(ref.shape) == 3 for i in range(ref.shape[0])] or list(refs)


def low_of(word):
    return (jnp.full((ROWS, LANES), word, jnp.int32) >> 7) & 255


def keep_of(word):
    return (jnp.full((ROWS, LANES), word, jnp.int32) >> 15) & 255


def rank_kernel(targets, tiles, t_ref, table_ref, rank_ref, place_ref):
    t = t_ref[...]
    me = first_target(targets)
    blocks = t.shape[0]
    rows = blocks + ROWS
    before = (iota((LANES, LANES), 0) <= iota((LANES, LANES), 1)).astype(jnp.float32)
    sums = jnp.concatenate([before, jnp.ones((LANES, LANES), jnp.float32)], 1).astype(jnp.bfloat16)
    earlier = (iota((rows, blocks), 1) < iota((rows, blocks), 0)).astype(jnp.float32).astype(jnp.bfloat16)
    lane = iota((1, LANES), 1)
    start = jnp.zeros((blocks, LANES), jnp.float32)
    rank = jnp.zeros((blocks, LANES), jnp.float32)
    place = jnp.zeros((blocks, LANES), jnp.float32)
    starts = jnp.zeros((blocks, LANES), jnp.float32)
    numbers = jnp.zeros((blocks, LANES), jnp.float32)
    offsets = jnp.zeros((rows, LANES), jnp.float32)
    for first in range(0, targets, GROUP):
        group = range(first, min(first + GROUP, targets))
        masks = [t == d for d in group]
        ones = jnp.concatenate([m.astype(jnp.float32) for m in masks], 0).astype(jnp.bfloat16)
        counted = jnp.dot(ones, sums, preferred_element_type=jnp.float32)
        totals = [counted[i * blocks:(i + 1) * blocks, LANES:] for i in range(len(masks))]
        based = jnp.dot(earlier, jnp.concatenate(totals, 1).astype(jnp.bfloat16), preferred_element_type=jnp.float32)
        for i, d in enumerate(group):
            inclusive = counted[i * blocks:(i + 1) * blocks, :LANES]
            base = based[:, i * LANES:(i + 1) * LANES]
            mine = lane % targets == d ^ me
            rank = jnp.where(masks[i], base[:blocks] + inclusive - 1.0, rank)
            place = jnp.where(masks[i], start + inclusive - 1.0, place)
            starts = jnp.where(mine, start, starts)
            numbers = jnp.where(mine, totals[i], numbers)
            offsets = jnp.where(mine, base, offsets)
            start = start + totals[i]
    pad = jnp.zeros((rows - blocks, LANES), jnp.int32)
    starts = jnp.concatenate([starts.astype(jnp.int32), pad], 0)
    numbers = jnp.concatenate([numbers.astype(jnp.int32), pad], 0)
    offsets = offsets.astype(jnp.int32)
    tile = jnp.minimum(offsets >> 7, tiles - 1)
    low = jnp.where(offsets == tiles * LANES, LANES, offsets & (LANES - 1))
    keep = jnp.where((low + numbers >= LANES) & (tile + 1 < tiles), 0, low)
    turn = (low - starts) & (LANES - 1)
    word = turn + (low << 7) + (keep << 15) + (tile << 23)
    word = jnp.concatenate([word, jnp.zeros((LANES - rows, LANES), jnp.int32)], 0)
    table_ref[...] = word.T[:table_ref.shape[0]]
    rank_ref[...] = rank.astype(jnp.int32)
    place_ref[...] = place.astype(jnp.int32)


def source_kernel(targets, table_ref, place_ref, mixing_ref, density_ref, *refs):
    slope_ref, outs = refs[0], blocks_of(refs[1:-3])
    sorted_ref, table_smem, table_sem = refs[-3:]
    levels, capacity = outs[0].shape
    blocks = place_ref.shape[0]
    load_table = pltpu.make_async_copy(table_ref, table_smem, table_sem)
    load_table.start()
    lanes_row = iota((ROWS, LANES), 1).astype(jnp.float32).astype(jnp.bfloat16)
    sublane = iota((LANES, LANES), 0)
    lane = iota((ROWS, LANES), 1)
    parts = range(0, levels, ROWS)
    for out in outs:
        out[...] = jnp.zeros((levels, capacity), jnp.float32)

    def reflect(j, carry):
        at = tile_at(j)
        rho = density_ref[:, at]
        total = jnp.zeros((levels, LANES), jnp.float32)
        for k in range(3):
            q = mixing_ref[k, :, at]
            powered = coefficients[k] * jnp.exp(exponents[k] * jnp.log(rho * q))
            total = total + powered
            slope_ref[k, :, at] = exponents[k] * powered / q
        chosen = (sublane == place_ref[pl.ds(j, 1), :]).astype(jnp.float32).astype(jnp.bfloat16)
        source = lax.dot_general(lanes_row, chosen, (((1,), (1,)), ((), ())), preferred_element_type=jnp.float32)
        source = source.astype(jnp.int32)
        for r in parts:
            sorted_ref[r:r + ROWS, at] = jnp.take_along_axis(total[r:r + ROWS], source, axis=1)
        return carry

    lax.fori_loop(0, blocks, reflect, 0, unroll=4)
    load_table.wait()

    def place_group(first, count):
        def step(j, held):
            values = [sorted_ref[r:r + ROWS, tile_at(j)] for r in parts]
            new = []
            for i in range(count):
                word = table_smem[first + i, j]
                low, keep, turn, at = low_of(word), keep_of(word), word & (LANES - 1), tile_at(word >> 23)
                for n, r in enumerate(parts):
                    turned = pltpu.roll(values[n], turn, 1)
                    out = refs[1].at[first + i] if targets > DIRECT else outs[i]
                    out[r:r + ROWS, at] = jnp.where(lane >= low, turned, held[i * len(parts) + n])
                    new.append(jnp.where(lane >= keep, turned, held[i * len(parts) + n]))
            return tuple(new)

        zero = jnp.zeros((ROWS, LANES), jnp.float32)
        held = lax.fori_loop(0, blocks, step, (zero,) * (count * len(parts)), unroll=2)
        for i in range(count):
            out = refs[1].at[first + i] if targets > DIRECT else outs[i]
            word = table_smem[first + i, blocks]
            for n, r in enumerate(parts):
                out[r:r + ROWS, tile_at(word >> 23)] = jnp.where(lane < low_of(word), held[i * len(parts) + n], 0.0)

    if targets <= GROUP:
        place_group(0, targets)
    else:
        @pl.loop(0, targets // GROUP)
        def _(g):
            place_group(g * GROUP, GROUP)


def pick_weights(w_ref, picked_ref, order, rows):
    gates = picked_ref.shape[-1]
    levels = picked_ref.shape[0] // len(order)
    for part in range(w_ref.shape[1] // gates):
        @pl.when(rows == part)
        def _():
            for i, l in enumerate(order):
                block = w_ref[pl.ds(pl.multiple_of(l * levels, levels), levels), :]
                picked_ref[i * levels:(i + 1) * levels, :] = block[:, part * gates:(part + 1) * gates]


def adjoint_kernel(targets, group, w_ref, own_ref, near_ref, *refs):
    out_refs, picked_ref = refs[:-1], refs[-1]
    levels, capacity = out_refs[0].shape[1:]
    me = first_target(targets)
    mine = lax.axis_index("lev")
    order = [mine ^ (2 * m) for m in range(len(out_refs))]
    for i in range(2):
        pick_weights(w_ref, picked_ref.at[i], order, mine ^ i)

    def step(s, carry):
        at = (group.start + group.step * s) ^ me
        at = pl.ds(pl.multiple_of(at * capacity, capacity), capacity)
        total = split_dot(picked_ref[0], own_ref[:, at]) + split_dot(picked_ref[1], near_ref[:, at])
        for i, out_ref in enumerate(out_refs):
            out_ref[s] = total[i * levels:(i + 1) * levels]
        return carry

    lax.fori_loop(0, len(group), step, 0)


def gate_part(targets, group, w_ref, sources, out_any, buffer, picked_ref, sem):
    mine = lax.axis_index("lev")
    half = len(sources) // 2
    order = [mine ^ (2 * (i % half)) ^ (i // half) for i in range(len(sources))]
    pick_weights(w_ref, picked_ref, order, mine)
    capacity = sources[0].shape[-1]
    me = first_target(targets)
    weights = picked_ref[...].T

    def column(s):
        return pl.ds(pl.multiple_of(((group.start + group.step * s) ^ me) * capacity, capacity), capacity)

    def store(s):
        part = pl.ds(pl.multiple_of(s * capacity, capacity), capacity)
        return pltpu.make_async_copy(buffer.at[:, part], out_any.at[:, column(s)], sem.at[s])

    def step(s, carry):
        part = pl.ds(pl.multiple_of(s * capacity, capacity), capacity)
        buffer[:, part] = split_dot(weights, jnp.concatenate([ref[s] for ref in sources], 0))
        store(s).start()
        return carry

    def finish(s, carry):
        store(s).wait()
        return carry

    lax.fori_loop(0, len(group), step, 0)
    return lambda: lax.fori_loop(0, len(group), finish, 0)


def increment_part(targets, table_ref, rank_ref, t_ref, slope_ref, refs, out_any, out_ref, sem):
    backs = blocks_of(refs)
    levels, capacity = backs[0].shape
    blocks = rank_ref.shape[0]
    tiles = capacity // LANES
    lane = iota((ROWS, LANES), 1)
    parts = range(0, levels, ROWS)
    me = first_target(targets)
    count = min(GROUP, targets)

    def block(j, carry):
        index = jnp.broadcast_to(rank_ref[pl.ds(j, 1), :] & (LANES - 1), (ROWS, LANES))
        target = jnp.broadcast_to(t_ref[pl.ds(j, 1), :], (ROWS, LANES)) ^ me

        def pick(first, found):
            found = list(found)
            for i in range(count):
                word = table_ref[first + i, j]
                low, tile = low_of(word), word >> 23
                later = jnp.minimum(tile + 1, tiles - 1)
                back = refs[0].at[first + i] if targets > DIRECT else backs[i]
                for n, r in enumerate(parts):
                    window = jnp.where(lane >= low, back[r:r + ROWS, tile_at(tile)], back[r:r + ROWS, tile_at(later)])
                    moved = jnp.take_along_axis(window, index, axis=1)
                    found[n] = jnp.where(target == first + i, moved, found[n])
            return tuple(found)

        found = (jnp.zeros((ROWS, LANES), jnp.float32),) * len(parts)
        if targets <= count:
            found = pick(0, found)
        else:
            found = lax.fori_loop(0, targets // count, lambda g, f: pick(g * count, f), found)
        for k in range(3):
            for n, r in enumerate(parts):
                out_ref[k, r:r + ROWS, tile_at(j)] = slope_ref[k, r:r + ROWS, tile_at(j)] * found[n]
        return carry

    pieces = sem.shape[0]
    stores = []
    for p in range(pieces):
        first, last = blocks * p // pieces, blocks * (p + 1) // pieces
        lax.fori_loop(first, last, block, 0, unroll=4)
        here = slice(first * LANES, last * LANES)
        stores.append(pltpu.make_async_copy(out_ref.at[:, :, here], out_any.at[:, :, here], sem.at[p]))
        stores[-1].start()
    return lambda: [store.wait() for store in stores]


def gate_kernel(targets, group, w_ref, *refs):
    out_any, buffer, picked_ref, sem = refs[-4:]
    sources = [ref for ref in refs[:-4] if len(ref.shape) == 3]
    gate_part(targets, group, w_ref, sources, out_any, buffer, picked_ref, sem)()


def final_kernel(targets, group, columns, backs, table_ref, rank_ref, t_ref, slope_ref, w_ref, *refs):
    sources, refs = refs[:columns], refs[columns:]
    returned, refs = refs[:backs], refs[backs:]
    gate_any, out_any, buffer, picked_ref, gate_sem, out_ref, out_sem = refs[-7:]
    gates_done = gate_part(targets, group, w_ref, sources, gate_any, buffer, picked_ref, gate_sem)
    increments_done = increment_part(
        targets, table_ref, rank_ref, t_ref, slope_ref, returned, out_any, out_ref, out_sem)
    gates_done()
    increments_done()


def settings(mib, micros):
    cost = pl.CostEstimate(flops=int(micros * 1e9), bytes_accessed=0, transcendentals=0)
    return dict(compiler_params=pltpu.CompilerParams(vmem_limit_bytes=mib << 20), cost_estimate=cost)


def full(space=pltpu.VMEM):
    return pl.BlockSpec(memory_space=space)


def per_device(mixing, density, routes, beam_weight, gate_adjoint):
    tile_count = lax.axis_size("tile")
    level_count = lax.axis_size("lev")
    level_dev, column_dev = density.shape
    capacity = 2 * column_dev // tile_count
    blocks = column_dev // LANES
    far = level_count // 2
    gate_dev = gate_adjoint.shape[0]
    direct = tile_count <= DIRECT
    f32, i32 = jnp.float32, jnp.int32
    shape = jax.ShapeDtypeStruct

    def swap(x, bits):
        return lax.ppermute(x, "lev", [(i, i ^ bits) for i in range(level_count)])

    def exchange(x, bits):
        return lax.ppermute(x, "tile", [(i, i ^ bits) for i in range(tile_count)])

    weights = beam_weight[0].T
    t = routes.reshape(blocks, LANES)
    table_shape = (max(tile_count, ROWS), LANES)
    half = tile_count // 2
    if direct:
        block_shapes = [shape((level_dev, capacity), f32)] * tile_count
        groups = [range(1, tile_count, 2), range(0, tile_count, 2)]
        sites = [range(0, half), range(half, tile_count)]
    else:
        block_shapes = [shape((tile_count, level_dev, capacity), f32)]
        groups = sites = [range(0, tile_count)]

    near_adjoint = swap(gate_adjoint, 1)
    table, rank, place = pl.pallas_call(
        functools.partial(rank_kernel, tile_count, capacity // LANES),
        out_shape=[shape(table_shape, i32)] + [shape((blocks, LANES), i32)] * 2,
        in_specs=[full()],
        out_specs=[full()] * 3,
        **settings(12, 1),
    )(t)
    slopes, *outgoing = pl.pallas_call(
        functools.partial(source_kernel, tile_count),
        out_shape=[shape(mixing.shape, f32)] + block_shapes,
        in_specs=[full()] * 4,
        out_specs=[full()] * (1 + len(block_shapes)),
        scratch_shapes=[
            pltpu.VMEM(density.shape, f32),
            pltpu.SMEM(table_shape, i32),
            pltpu.SemaphoreType.DMA,
        ],
        **settings(12, 4),
    )(table, place, mixing, density)

    partial = []
    for group in groups:
        partial.append(pl.pallas_call(
            functools.partial(adjoint_kernel, tile_count, group),
            out_shape=[shape((len(group), level_dev, capacity), f32)] * far,
            in_specs=[full()] * 3,
            out_specs=[full()] * far,
            scratch_shapes=[pltpu.VMEM((2, far * level_dev, gate_dev), f32)],
            **settings(12, 2),
        )(weights, gate_adjoint, near_adjoint))

    totals = []
    for parts in partial:
        total = parts[0]
        for m in range(1, far):
            part = swap(parts[m], 2 * m)
            total = total + part
        totals.append(total)
    if direct:
        incoming = [outgoing[0]]
        for k in range(1, tile_count):
            incoming.append(exchange(outgoing[k], k))
        arrived = []
        for site in sites:
            arrived.append(jnp.stack([incoming[k] for k in site]))
        crossed = exchange(totals[0], 1)
        restored = []
        for p in range(half):
            pair = jnp.stack([totals[1][p], crossed[p]])
            restored.append(pair if p == 0 else exchange(pair, 2 * p))
    else:
        arrived = [lax.all_to_all(outgoing[0], "tile", split_axis=0, concat_axis=0, tiled=True)]
        restored = [lax.all_to_all(totals[0], "tile", split_axis=0, concat_axis=0, tiled=True)]

    gate_values = None
    for n, (group, here) in enumerate(zip(sites, arrived)):
        columns = [here]
        for m in range(1, far):
            columns.append(swap(here, 2 * m))
        for m in range(far):
            columns.append(swap(columns[m], 1))
        before = [] if gate_values is None else [gate_values]
        gate_scratch = [
            pltpu.VMEM((gate_dev, len(group) * capacity), f32),
            pltpu.VMEM(weights.shape[:1] + (gate_dev,), f32),
            pltpu.SemaphoreType.DMA((len(group),)),
        ]
        if n + 1 < len(sites):
            gate_values = pl.pallas_call(
                functools.partial(gate_kernel, tile_count, group),
                out_shape=shape(gate_adjoint.shape, f32),
                in_specs=[full()] * (1 + len(columns)) + [full(pltpu.HBM)] * len(before),
                out_specs=full(pltpu.HBM),
                input_output_aliases={1 + len(columns): 0} if before else {},
                scratch_shapes=gate_scratch,
                **settings(12, 2),
            )(weights, *columns, *before)
            continue
        operands = [table, rank, t, slopes, weights, *columns, *restored]
        gate_values, increments = pl.pallas_call(
            functools.partial(final_kernel, tile_count, group, len(columns), len(restored)),
            out_shape=[shape(gate_adjoint.shape, f32), shape(mixing.shape, f32)],
            in_specs=[full(SMEM)] + [full()] * (len(operands) - 1) + [full(pltpu.HBM)] * len(before),
            out_specs=[full(pltpu.HBM)] * 2,
            input_output_aliases={len(operands): 0} if before else {},
            scratch_shapes=gate_scratch + [pltpu.VMEM(mixing.shape, f32), pltpu.SemaphoreType.DMA((4,))],
            **settings(16, 4),
        )(*operands, *before)
    return gate_values, increments


def solution(mesh):
    return jax.shard_map(
        per_device,
        mesh=mesh,
        in_specs=(
            P(None, "lev", "tile"),
            P("lev", "tile"),
            P("tile", None),
            P("tile", None, None),
            P("lev", "tile"),
        ),
        out_specs=(P("lev", "tile"), P(None, "lev", "tile")),
        check_vma=False,
    )
```

profile of v0, /device:TPU:0, one launch (start us, length us, event | category | flops | bytes accessed | tf_op | source)
XLA Modules:
  0.0 65.5 jit_solution(14836706096976922038)
XLA Ops:
  0.6 0.6 collective-permute-start.7
  1.2 0.0 copy-start.4
  1.2 0.7 %copy-done.4 = s32[4096,1]{0,1:T(1,128)S(1)} copy-done((s32[4096,1]{0,1:T(1,128)S(1)}, s32[4096,1]{0,1:T(1,128)}, u32[]{:S(2)}) %copy-start.4) | copy-done | bytes 16408
  1.9 0.0 copy-start.1
  1.9 0.0 copy-start.2
  1.9 0.4 shard_map.68
  2.3 0.7 %copy-done.1 = f32[3,16,4096]{2,1,0:T(8,128)S(1)} copy-done((f32[3,16,4096]{2,1,0:T(8,128)S(1)}, f32[3,16,4096]{2,1,0:T(8,128)}, u32[]{:S(2)}) %copy-start.1) | copy-done | bytes 786456
  3.0 0.1 copy-done.2
  3.1 0.0 copy-start
  3.1 0.0 copy-start.3
  3.1 3.8 %shard_map.69 = (f32[3,16,4096]{2,1,0:T(8,128)S(1)}, f32[16,1024]{1,0:T(8,128)S(1)}, f32[16,1024]{1,0:T(8,128)S(1)}, f32[16,1024]{1,0:T(8,128)S(1)}, f32[16,1024...) custom-call(s32[8,128]{1,0:T(8,128)S(1)} %get-tuple-element.18.table, ...), custom_call_target="tpu_custom_call" | custom-call | flops 4000000000 | tf_op jit(solution)/shard_map/pallas_call | solution.py:341
  6.9 2.6 %collective-permute-start.14 = (f32[16,1024]{1,0:T(8,128)S(1)}, f32[16,1024]{1,0:T(8,128)S(1)}, u32[]{:S(2)}, u32[]{:S(2)}) collective-permute-start(f32[16,1024]{1,0:T(8,128)S(1)} %get-tuple-element.31), channel_id=1, source_target_pairs={{0,4},{4,0},{8,12},{12,8},{16,20},{20,16},{24,28},{28,24},{1,5},{5... | collective-permute-start | bytes 196616 | tf_op jit(solution)/shard_map/ppermute | solution.py:319
  9.5 1.6 %collective-permute-start.15 = (f32[16,1024]{1,0:T(8,128)S(1)}, f32[16,1024]{1,0:T(8,128)S(1)}, u32[]{:S(2)}, u32[]{:S(2)}) collective-permute-start(f32[16,1024]{1,0:T(8,128)S(1)} %get-tuple-element.32), channel_id=1, source_target_pairs={{0,8},{4,12},{8,0},{12,4},{16,24},{20,28},{24,16},{28,20},{1,9},{5... | collective-permute-start | bytes 196616 | tf_op jit(solution)/shard_map/ppermute | solution.py:319
  11.1 0.0 collective-permute-start.16
  11.1 3.0 %collective-permute-start = (f32[16,1024]{1,0:T(8,128)S(1)}, f32[16,1024]{1,0:T(8,128)S(1)}, u32[]{:S(2)}, u32[]{:S(2)}) collective-permute-start(f32[16,1024]{1,0:T(8,128)S(1)} %get-tuple-element.22), channel_id=1, source_target_pairs={{0,16},{4,20},{8,24},{12,28},{16,0},{20,4},{24,8},{28,12},{1,17},{... | collective-permute-start | bytes 196616 | tf_op jit(solution)/shard_map/ppermute | solution.py:319
  14.1 0.0 collective-permute-done.14
  14.1 1.9 %collective-permute-start.1 = (f32[16,1024]{1,0:T(8,128)S(1)}, f32[16,1024]{1,0:T(8,128)S(1)}, u32[]{:S(2)}, u32[]{:S(2)}) collective-permute-start(f32[16,1024]{1,0:T(8,128)S(1)} %get-tuple-element.23), channel_id=1, source_target_pairs={{0,20},{4,16},{8,28},{12,24},{16,4},{20,0},{24,12},{28,8},{1,21},{... | collective-permute-start | bytes 196616 | tf_op jit(solution)/shard_map/ppermute | solution.py:319
  16.0 0.0 collective-permute-done.15
  16.0 2.9 %collective-permute-start.2 = (f32[16,1024]{1,0:T(8,128)S(1)}, f32[16,1024]{1,0:T(8,128)S(1)}, u32[]{:S(2)}, u32[]{:S(2)}) collective-permute-start(f32[16,1024]{1,0:T(8,128)S(1)} %get-tuple-element.24), channel_id=1, source_target_pairs={{0,24},{4,28},{8,16},{12,20},{16,8},{20,12},{24,0},{28,4},{1,25},{... | collective-permute-start | bytes 196616 | tf_op jit(solution)/shard_map/ppermute | solution.py:319
  18.9 0.0 collective-permute-done.16
  18.9 1.1 %collective-permute-start.3 = (f32[16,1024]{1,0:T(8,128)S(1)}, f32[16,1024]{1,0:T(8,128)S(1)}, u32[]{:S(2)}, u32[]{:S(2)}) collective-permute-start(f32[16,1024]{1,0:T(8,128)S(1)} %get-tuple-element.25), channel_id=1, source_target_pairs={{0,28},{4,24},{8,20},{12,16},{16,12},{20,8},{24,4},{28,0},{1,29},{... | collective-permute-start | bytes 196616 | tf_op jit(solution)/shard_map/ppermute | solution.py:319
  20.0 0.0 collective-permute-done
  20.0 1.6 %collective-permute-start.17 = (f32[4,16,1024]{2,1,0:T(8,128)S(1)}, f32[4,16,1024]{2,1,0:T(8,128)S(1)}, u32[]{:S(2)}, u32[]{:S(2)}) collective-permute-start(f32[4,16,1024]{2,1,0:T(8,128)S(1)} %pad_maximum_fusion.1.refs_0_), channel_id=1, source_target_pairs={{0,2},{1,3},{2,0},{3,1},{4,6},{5,7},{6,4},{7,5},{8,10},{9,11},{10,... | collective-permute-start | bytes 786440 | tf_op jit(solution)/shard_map/ppermute | solution.py:316
  21.6 2.6 %collective-permute-done.1 = f32[16,1024]{1,0:T(8,128)S(1)} collective-permute-done((f32[16,1024]{1,0:T(8,128)S(1)}, f32[16,1024]{1,0:T(8,128)S(1)}, u32[]{:S(2)}, u32[]{:S(2)}) %collective-permute-start.1) | collective-permute-done | bytes 65568 | tf_op jit(solution)/shard_map/ppermute | solution.py:319
  24.2 0.0 collective-permute-done.2
  24.2 1.8 %collective-permute-done.3 = f32[16,1024]{1,0:T(8,128)S(1)} collective-permute-done((f32[16,1024]{1,0:T(8,128)S(1)}, f32[16,1024]{1,0:T(8,128)S(1)}, u32[]{:S(2)}, u32[]{:S(2)}) %collective-permute-start.3) | collective-permute-done | bytes 65568 | tf_op jit(solution)/shard_map/ppermute | solution.py:319
  26.0 1.6 %collective-permute-start.4 = (f32[4,16,1024]{2,1,0:T(8,128)S(1)}, f32[4,16,1024]{2,1,0:T(8,128)S(1)}, u32[]{:S(2)}, u32[]{:S(2)}) collective-permute-start(f32[4,16,1024]{2,1,0:T(8,128)S(1)} %pad_maximum_fusion.refs_0_), channel_id=1, source_target_pairs={{0,2},{1,3},{2,0},{3,1},{4,6},{5,7},{6,4},{7,5},{8,10},{9,11},{10,... | collective-permute-start | bytes 786440 | tf_op jit(solution)/shard_map/ppermute | solution.py:316
  27.6 0.0 collective-permute-done.7.near_ref
  27.6 0.0 copy-done
  27.6 0.0 copy-done.3
  27.6 1.1 %shard_map.71 = (f32[4,16,1024]{2,1,0:T(8,128)S(1)}, f32[4,16,1024]{2,1,0:T(8,128)S(1)}) custom-call(f32[64,168]{1,0:T(8,128)S(1)} %bitcast.13, f32[42,8192]{1,0:T(8,128)S(1)} %copy-done, f32[42,8192]{1,0:T(8,128)S(1)} %collective-permute-done.7.near_ref), custom_call_target="tpu_custom_call" | custom-call | flops 2000000000 | tf_op jit(solution)/shard_map/pallas_call | solution.py:356
  28.7 0.6 collective-permute-start.9
  29.4 1.1 %shard_map.70 = (f32[4,16,1024]{2,1,0:T(8,128)S(1)}, f32[4,16,1024]{2,1,0:T(8,128)S(1)}) custom-call(f32[64,168]{1,0:T(8,128)S(1)} %bitcast.14, f32[42,8192]{1,0:T(8,128)S(1)} %copy-done, f32[42,8192]{1,0:T(8,128)S(1)} %collective-permute-done.7.near_ref), custom_call_target="tpu_custom_call" | custom-call | flops 2000000000 | tf_op jit(solution)/shard_map/pallas_call | solution.py:356
  30.5 1.6 %collective-permute-start.8 = (f32[4,16,1024]{2,1,0:T(8,128)S(1)}, f32[4,16,1024]{2,1,0:T(8,128)S(1)}, u32[]{:S(2)}, u32[]{:S(2)}) collective-permute-start(f32[4,16,1024]{2,1,0:T(8,128)S(1)} %get-tuple-element.27), channel_id=1, source_target_pairs={{0,2},{1,3},{2,0},{3,1},{4,6},{5,7},{6,4},{7,5},{8,10},{9,11},{10,... | collective-permute-start | bytes 786440 | tf_op jit(solution)/shard_map/ppermute | solution.py:316
  32.1 8.8 %collective-permute-done.9 = f32[4,16,1024]{2,1,0:T(8,128)S(1)} collective-permute-done((f32[4,16,1024]{2,1,0:T(8,128)S(1)}, f32[4,16,1024]{2,1,0:T(8,128)S(1)}, u32[]{:S(2)}, u32[]{:S(2)}) %collective-permute-start.9) | collective-permute-done | bytes 262176 | tf_op jit(solution)/shard_map/ppermute | solution.py:316
  40.9 0.6 collective-permute-start.10
  41.5 0.0 collective-permute-start.18
  41.5 0.0 collective-permute-done.17.refs_1_
  41.5 0.5 collective-permute-start.5
  42.0 0.0 collective-permute-done.4.refs_1_
  42.1 0.1 collective-permute-start.19
  42.1 1.6 %collective-permute-done.8 = f32[4,16,1024]{2,1,0:T(8,128)S(1)} collective-permute-done((f32[4,16,1024]{2,1,0:T(8,128)S(1)}, f32[4,16,1024]{2,1,0:T(8,128)S(1)}, u32[]{:S(2)}, u32[]{:S(2)}) %collective-permute-start.8) | collective-permute-done | bytes 262176 | tf_op jit(solution)/shard_map/ppermute | solution.py:316
  43.8 0.0 collective-permute-start.6
  43.8 3.5 %collective-permute-done.10 = f32[4,16,1024]{2,1,0:T(8,128)S(1)} collective-permute-done((f32[4,16,1024]{2,1,0:T(8,128)S(1)}, f32[4,16,1024]{2,1,0:T(8,128)S(1)}, u32[]{:S(2)}, u32[]{:S(2)}) %collective-permute-start.10) | collective-permute-done | bytes 262176 | tf_op jit(solution)/shard_map/ppermute | solution.py:319
  47.4 2.0 %collective-permute-start.11 = (f32[2,16,1024]{2,1,0:T(8,128)S(1)}, f32[2,16,1024]{2,1,0:T(8,128)S(1)}, u32[]{:S(2)}, u32[]{:S(2)}) collective-permute-start(f32[2,16,1024]{2,1,0:T(8,128)S(1)} %pad_maximum_fusion.3), channel_id=1, source_target_pairs={{0,8},{4,12},{8,0},{12,4},{16,24},{20,28},{24,16},{28,20},{1,9},{5... | collective-permute-start | bytes 393224 | tf_op jit(solution)/shard_map/ppermute | solution.py:319
  49.5 0.0 copy-start.5
  49.5 0.0 collective-permute-done.18.refs_2_
  49.5 1.8 %collective-permute-start.12 = (f32[2,16,1024]{2,1,0:T(8,128)S(1)}, f32[2,16,1024]{2,1,0:T(8,128)S(1)}, u32[]{:S(2)}, u32[]{:S(2)}) collective-permute-start(f32[2,16,1024]{2,1,0:T(8,128)S(1)} %pad_maximum_fusion.4), channel_id=1, source_target_pairs={{0,16},{4,20},{8,24},{12,28},{16,0},{20,4},{24,8},{28,12},{1,17},{... | collective-permute-start | bytes 393224 | tf_op jit(solution)/shard_map/ppermute | solution.py:319
  51.3 0.0 collective-permute-done.19.refs_3_
  51.3 1.2 %collective-permute-start.13 = (f32[2,16,1024]{2,1,0:T(8,128)S(1)}, f32[2,16,1024]{2,1,0:T(8,128)S(1)}, u32[]{:S(2)}, u32[]{:S(2)}) collective-permute-start(f32[2,16,1024]{2,1,0:T(8,128)S(1)} %pad_maximum_fusion.5), channel_id=1, source_target_pairs={{0,24},{4,28},{8,16},{12,20},{16,8},{20,12},{24,0},{28,4},{1,25},{... | collective-permute-start | bytes 393224 | tf_op jit(solution)/shard_map/ppermute | solution.py:319
  52.5 1.8 %shard_map.72.refs_8_ = f32[42,8192]{1,0:T(8,128)} custom-call(f32[64,168]{1,0:T(8,128)S(1)} %bitcast.15, f32[4,16,1024]{2,1,0:T(8,128)S(1)} %pad_maximum_fusion.1.refs_0_, f32[4,16,1024]{2,1,0:T(8,128)S(1)} %collective-permute-done.17.refs_1_, f32[4,16,1024]{2,1,0:T(8,128)S(1)} %collective-permute-done.18.refs_2_, ...), custom_call_target="tpu_custom_call" | custom-call | flops 2000000000 | tf_op jit(solution)/shard_map/pallas_call | solution.py:402
  54.3 0.0 collective-permute-done.5.refs_2_
  54.3 0.0 collective-permute-done.6.refs_3_
  54.3 0.0 collective-permute-done.11.refs_5_
  54.3 7.0 %collective-permute-done.12.refs_6_ = f32[2,16,1024]{2,1,0:T(8,128)S(1)} collective-permute-done((f32[2,16,1024]{2,1,0:T(8,128)S(1)}, f32[2,16,1024]{2,1,0:T(8,128)S(1)}, u32[]{:S(2)}, u32[]{:S(2)}) %collective-permute-start.12) | collective-permute-done | bytes 131104 | tf_op jit(solution)/shard_map/ppermute | solution.py:319
  61.3 0.0 collective-permute-done.13.refs_7_
  61.3 0.0 copy-done.5
  61.3 4.1 %shard_map.73 = (f32[42,8192]{1,0:T(8,128)}, f32[3,16,4096]{2,1,0:T(8,128)}) custom-call(s32[8,128]{1,0:T(8,128)S(1)} %get-tuple-element.18.table_ref, s32[32,128]{1,0:T(8,128)S(1)} %get-tuple-element.19.rank_ref, s32[32,128]{1,0:T(8,128)S(1)} %bitcast.18, f32[3,16,4096]{2,1,0:T(8,128)S(1)} %get-tuple-element.21.slope_ref, ...), custom_call_target="tpu_custom_call", output_to_operand_aliasing={{0}: (13, {})} | custom-call | flops 4000000000 | tf_op jit(solution)/shard_map/pallas_call | solution.py:413
  (10 shorter events, 0.2 us)
Async XLA Ops:
  0.6 27.0 %collective-permute-start.7 = (f32[42,8192]{1,0:T(8,128)}, f32[42,8192]{1,0:T(8,128)S(1)}, u32[]{:S(2)}, u32[]{:S(2)}) collective-permute-start(f32[42,8192]{1,0:T(8,128)} %own_ref.3), channel_id=1, source_target_pairs={{0,1},{1,0},{2,3},{3,2},{4,5},{5,4},{6,7},{7,6},{8,9},{9,8},{10,11... | collective-permute-start | bytes 4128776 | tf_op jit(solution)/shard_map/ppermute | solution.py:316
  1.2 0.7 %copy-start.4 = (s32[4096,1]{0,1:T(1,128)S(1)}, s32[4096,1]{0,1:T(1,128)}, u32[]{:S(2)}) copy-start(s32[4096,1]{0,1:T(1,128)} %param.7) | copy-start | bytes 49156
  1.9 1.1 %copy-start.1 = (f32[3,16,4096]{2,1,0:T(8,128)S(1)}, f32[3,16,4096]{2,1,0:T(8,128)}, u32[]{:S(2)}) copy-start(f32[3,16,4096]{2,1,0:T(8,128)} %mixing_ref.1) | copy-start | bytes 2359300
  1.9 1.2 %copy-start.2 = (f32[16,4096]{1,0:T(8,128)S(1)}, f32[16,4096]{1,0:T(8,128)}, u32[]{:S(2)}) copy-start(f32[16,4096]{1,0:T(8,128)} %density_ref.1) | copy-start | bytes 786436
  3.1 24.5 %copy-start = (f32[42,8192]{1,0:T(8,128)S(1)}, f32[42,8192]{1,0:T(8,128)}, u32[]{:S(2)}) copy-start(f32[42,8192]{1,0:T(8,128)} %own_ref.3) | copy-start | bytes 4128772
  3.1 24.5 %copy-start.3 = (f32[1,168,64]{1,2,0:T(8,128)S(1)}, f32[1,168,64]{1,2,0:T(8,128)}, u32[]{:S(2)}) copy-start(f32[1,168,64]{1,2,0:T(8,128)} %param.8) | copy-start | bytes 129028
  6.9 7.1 %collective-permute-start.14 = (f32[16,1024]{1,0:T(8,128)S(1)}, f32[16,1024]{1,0:T(8,128)S(1)}, u32[]{:S(2)}, u32[]{:S(2)}) collective-permute-start(f32[16,1024]{1,0:T(8,128)S(1)} %get-tuple-element.31), channel_id=1, source_target_pairs={{0,4},{4,0},{8,12},{12,8},{16,20},{20,16},{24,28},{28,24},{1,5},{5... | collective-permute-start | bytes 196616 | tf_op jit(solution)/shard_map/ppermute | solution.py:319
  9.5 6.5 %collective-permute-start.15 = (f32[16,1024]{1,0:T(8,128)S(1)}, f32[16,1024]{1,0:T(8,128)S(1)}, u32[]{:S(2)}, u32[]{:S(2)}) collective-permute-start(f32[16,1024]{1,0:T(8,128)S(1)} %get-tuple-element.32), channel_id=1, source_target_pairs={{0,8},{4,12},{8,0},{12,4},{16,24},{20,28},{24,16},{28,20},{1,9},{5... | collective-permute-start | bytes 196616 | tf_op jit(solution)/shard_map/ppermute | solution.py:319
  11.1 7.9 %collective-permute-start.16 = (f32[16,1024]{1,0:T(8,128)S(1)}, f32[16,1024]{1,0:T(8,128)S(1)}, u32[]{:S(2)}, u32[]{:S(2)}) collective-permute-start(f32[16,1024]{1,0:T(8,128)S(1)} %get-tuple-element.33), channel_id=1, source_target_pairs={{0,12},{4,8},{8,4},{12,0},{16,28},{20,24},{24,20},{28,16},{1,13},{... | collective-permute-start | bytes 196616 | tf_op jit(solution)/shard_map/ppermute | solution.py:319
  11.1 9.0 %collective-permute-start = (f32[16,1024]{1,0:T(8,128)S(1)}, f32[16,1024]{1,0:T(8,128)S(1)}, u32[]{:S(2)}, u32[]{:S(2)}) collective-permute-start(f32[16,1024]{1,0:T(8,128)S(1)} %get-tuple-element.22), channel_id=1, source_target_pairs={{0,16},{4,20},{8,24},{12,28},{16,0},{20,4},{24,8},{28,12},{1,17},{... | collective-permute-start | bytes 196616 | tf_op jit(solution)/shard_map/ppermute | solution.py:319
  14.1 10.2 %collective-permute-start.1 = (f32[16,1024]{1,0:T(8,128)S(1)}, f32[16,1024]{1,0:T(8,128)S(1)}, u32[]{:S(2)}, u32[]{:S(2)}) collective-permute-start(f32[16,1024]{1,0:T(8,128)S(1)} %get-tuple-element.23), channel_id=1, source_target_pairs={{0,20},{4,16},{8,28},{12,24},{16,4},{20,0},{24,12},{28,8},{1,21},{... | collective-permute-start | bytes 196616 | tf_op jit(solution)/shard_map/ppermute | solution.py:319
  16.0 8.2 %collective-permute-start.2 = (f32[16,1024]{1,0:T(8,128)S(1)}, f32[16,1024]{1,0:T(8,128)S(1)}, u32[]{:S(2)}, u32[]{:S(2)}) collective-permute-start(f32[16,1024]{1,0:T(8,128)S(1)} %get-tuple-element.24), channel_id=1, source_target_pairs={{0,24},{4,28},{8,16},{12,20},{16,8},{20,12},{24,0},{28,4},{1,25},{... | collective-permute-start | bytes 196616 | tf_op jit(solution)/shard_map/ppermute | solution.py:319
  18.9 7.1 %collective-permute-start.3 = (f32[16,1024]{1,0:T(8,128)S(1)}, f32[16,1024]{1,0:T(8,128)S(1)}, u32[]{:S(2)}, u32[]{:S(2)}) collective-permute-start(f32[16,1024]{1,0:T(8,128)S(1)} %get-tuple-element.25), channel_id=1, source_target_pairs={{0,28},{4,24},{8,20},{12,16},{16,12},{20,8},{24,4},{28,0},{1,29},{... | collective-permute-start | bytes 196616 | tf_op jit(solution)/shard_map/ppermute | solution.py:319
  20.0 21.5 %collective-permute-start.17 = (f32[4,16,1024]{2,1,0:T(8,128)S(1)}, f32[4,16,1024]{2,1,0:T(8,128)S(1)}, u32[]{:S(2)}, u32[]{:S(2)}) collective-permute-start(f32[4,16,1024]{2,1,0:T(8,128)S(1)} %pad_maximum_fusion.1.refs_0_), channel_id=1, source_target_pairs={{0,2},{1,3},{2,0},{3,1},{4,6},{5,7},{6,4},{7,5},{8,10},{9,11},{10,... | collective-permute-start | bytes 786440 | tf_op jit(solution)/shard_map/ppermute | solution.py:316
  26.0 16.0 %collective-permute-start.4 = (f32[4,16,1024]{2,1,0:T(8,128)S(1)}, f32[4,16,1024]{2,1,0:T(8,128)S(1)}, u32[]{:S(2)}, u32[]{:S(2)}) collective-permute-start(f32[4,16,1024]{2,1,0:T(8,128)S(1)} %pad_maximum_fusion.refs_0_), channel_id=1, source_target_pairs={{0,2},{1,3},{2,0},{3,1},{4,6},{5,7},{6,4},{7,5},{8,10},{9,11},{10,... | collective-permute-start | bytes 786440 | tf_op jit(solution)/shard_map/ppermute | solution.py:316
  28.7 12.1 %collective-permute-start.9 = (f32[4,16,1024]{2,1,0:T(8,128)S(1)}, f32[4,16,1024]{2,1,0:T(8,128)S(1)}, u32[]{:S(2)}, u32[]{:S(2)}) collective-permute-start(f32[4,16,1024]{2,1,0:T(8,128)S(1)} %get-tuple-element.29), channel_id=1, source_target_pairs={{0,2},{1,3},{2,0},{3,1},{4,6},{5,7},{6,4},{7,5},{8,10},{9,11},{10,... | collective-permute-start | bytes 786440 | tf_op jit(solution)/shard_map/ppermute | solution.py:316
  30.5 13.3 %collective-permute-start.8 = (f32[4,16,1024]{2,1,0:T(8,128)S(1)}, f32[4,16,1024]{2,1,0:T(8,128)S(1)}, u32[]{:S(2)}, u32[]{:S(2)}) collective-permute-start(f32[4,16,1024]{2,1,0:T(8,128)S(1)} %get-tuple-element.27), channel_id=1, source_target_pairs={{0,2},{1,3},{2,0},{3,1},{4,6},{5,7},{6,4},{7,5},{8,10},{9,11},{10,... | collective-permute-start | bytes 786440 | tf_op jit(solution)/shard_map/ppermute | solution.py:316
  40.9 6.4 %collective-permute-start.10 = (f32[4,16,1024]{2,1,0:T(8,128)S(1)}, f32[4,16,1024]{2,1,0:T(8,128)S(1)}, u32[]{:S(2)}, u32[]{:S(2)}) collective-permute-start(f32[4,16,1024]{2,1,0:T(8,128)S(1)} %add.7), channel_id=1, source_target_pairs={{0,4},{4,0},{8,12},{12,8},{16,20},{20,16},{24,28},{28,24},{1,5},{5... | collective-permute-start | bytes 786440 | tf_op jit(solution)/shard_map/ppermute | solution.py:319
  41.5 7.9 %collective-permute-start.18 = (f32[4,16,1024]{2,1,0:T(8,128)S(1)}, f32[4,16,1024]{2,1,0:T(8,128)S(1)}, u32[]{:S(2)}, u32[]{:S(2)}) collective-permute-start(f32[4,16,1024]{2,1,0:T(8,128)S(1)} %pad_maximum_fusion.1.refs_0_), channel_id=1, source_target_pairs={{0,1},{1,0},{2,3},{3,2},{4,5},{5,4},{6,7},{7,6},{8,9},{9,8},{10,11... | collective-permute-start | bytes 786440 | tf_op jit(solution)/shard_map/ppermute | solution.py:316
  41.5 12.8 %collective-permute-start.5 = (f32[4,16,1024]{2,1,0:T(8,128)S(1)}, f32[4,16,1024]{2,1,0:T(8,128)S(1)}, u32[]{:S(2)}, u32[]{:S(2)}) collective-permute-start(f32[4,16,1024]{2,1,0:T(8,128)S(1)} %pad_maximum_fusion.refs_0_), channel_id=1, source_target_pairs={{0,1},{1,0},{2,3},{3,2},{4,5},{5,4},{6,7},{7,6},{8,9},{9,8},{10,11... | collective-permute-start | bytes 786440 | tf_op jit(solution)/shard_map/ppermute | solution.py:316
  42.1 9.3 %collective-permute-start.19 = (f32[4,16,1024]{2,1,0:T(8,128)S(1)}, f32[4,16,1024]{2,1,0:T(8,128)S(1)}, u32[]{:S(2)}, u32[]{:S(2)}) collective-permute-start(f32[4,16,1024]{2,1,0:T(8,128)S(1)} %collective-permute-done.17.refs_1_), channel_id=1, source_target_pairs={{0,1},{1,0},{2,3},{3,2},{4,5},{5,4},{6,7},{7,6},{8,9},{9,8},{10,11... | collective-permute-start | bytes 786440 | tf_op jit(solution)/shard_map/ppermute | solution.py:316
  43.8 10.6 %collective-permute-start.6 = (f32[4,16,1024]{2,1,0:T(8,128)S(1)}, f32[4,16,1024]{2,1,0:T(8,128)S(1)}, u32[]{:S(2)}, u32[]{:S(2)}) collective-permute-start(f32[4,16,1024]{2,1,0:T(8,128)S(1)} %collective-permute-done.4.refs_1_), channel_id=1, source_target_pairs={{0,1},{1,0},{2,3},{3,2},{4,5},{5,4},{6,7},{7,6},{8,9},{9,8},{10,11... | collective-permute-start | bytes 786440 | tf_op jit(solution)/shard_map/ppermute | solution.py:316
  47.4 6.9 %collective-permute-start.11 = (f32[2,16,1024]{2,1,0:T(8,128)S(1)}, f32[2,16,1024]{2,1,0:T(8,128)S(1)}, u32[]{:S(2)}, u32[]{:S(2)}) collective-permute-start(f32[2,16,1024]{2,1,0:T(8,128)S(1)} %pad_maximum_fusion.3), channel_id=1, source_target_pairs={{0,8},{4,12},{8,0},{12,4},{16,24},{20,28},{24,16},{28,20},{1,9},{5... | collective-permute-start | bytes 393224 | tf_op jit(solution)/shard_map/ppermute | solution.py:319
  49.5 11.9 %copy-start.5 = (s32[4096,1]{0,1:T(1,128)S(1)}, s32[4096,1]{0,1:T(1,128)}, u32[]{:S(2)}) copy-start(s32[4096,1]{0,1:T(1,128)} %param.7) | copy-start | bytes 49156
  49.5 11.8 %collective-permute-start.12 = (f32[2,16,1024]{2,1,0:T(8,128)S(1)}, f32[2,16,1024]{2,1,0:T(8,128)S(1)}, u32[]{:S(2)}, u32[]{:S(2)}) collective-permute-start(f32[2,16,1024]{2,1,0:T(8,128)S(1)} %pad_maximum_fusion.4), channel_id=1, source_target_pairs={{0,16},{4,20},{8,24},{12,28},{16,0},{20,4},{24,8},{28,12},{1,17},{... | collective-permute-start | bytes 393224 | tf_op jit(solution)/shard_map/ppermute | solution.py:319
  51.3 10.0 %collective-permute-start.13 = (f32[2,16,1024]{2,1,0:T(8,128)S(1)}, f32[2,16,1024]{2,1,0:T(8,128)S(1)}, u32[]{:S(2)}, u32[]{:S(2)}) collective-permute-start(f32[2,16,1024]{2,1,0:T(8,128)S(1)} %pad_maximum_fusion.5), channel_id=1, source_target_pairs={{0,24},{4,28},{8,16},{12,20},{16,8},{20,12},{24,0},{28,4},{1,25},{... | collective-permute-start | bytes 393224 | tf_op jit(solution)/shard_map/ppermute | solution.py:319
where the time goes:
time: 65.7 us; the launch traced here: 65.5 us
  waiting for transfers between devices  25.4 us (39%)
  starting transfers between devices  25.3 us (39%)
  Pallas kernels  12.3 us (19%)
  local copies, waits for them, and re-layouts  1.55 us (2%)
  between operations  0.78 us (1%)
    ppermute x11, starting transfers between devices, exchange(): return lax.ppermute(x, 'tile', [(i, i ^ bits) for i in range(tile_count)])  18.7 us
    ppermute x11, waiting for transfers between devices, exchange(): return lax.ppermute(x, 'tile', [(i, i ^ bits) for i in range(tile_count)])  14.9 us
    ppermute x9, waiting for transfers between devices, swap(): return lax.ppermute(x, 'lev', [(i, i ^ bits) for i in range(level_count)])  10.5 us
    ppermute x9, starting transfers between devices, swap(): return lax.ppermute(x, 'lev', [(i, i ^ bits) for i in range(level_count)])  6.54 us
    pallas_call x1, Pallas kernels, per_device(): pl.pallas_call(functools.partial(final_kernel, tile_count, group, len(col...  4.12 us
    pallas_call x1, Pallas kernels, per_device(): pl.pallas_call(functools.partial(source_kernel, tile_count), out_shape=[s...  3.82 us
    pallas_call x2, Pallas kernels, per_device(): pl.pallas_call(functools.partial(adjoint_kernel, tile_count, group), out_...  2.19 us
    pallas_call x1, Pallas kernels, per_device(): pl.pallas_call(functools.partial(gate_kernel, tile_count, group), out_sha...  1.77 us
  transfers between devices with their start and end apart: 20, of which 6 were waited for; matrix products, arithmetic and copies ran while one was open for 0% of the time, Pallas kernels for 12%

commit v1 on v0

--- a/solution.py
+++ b/solution.py
@@ -21,6 +21,8 @@
 
 
 def tile_at(index):
+    if isinstance(index, int):
+        return slice(index * LANES, (index + 1) * LANES)
     return pl.ds(pl.multiple_of(index * LANES, LANES), LANES)
 
 
@@ -45,6 +47,10 @@
 
 def blocks_of(refs):
     return [ref.at[i] for ref in refs if len(ref.shape) == 3 for i in range(ref.shape[0])] or list(refs)
+
+
+def tile_of(word):
+    return (word >> 23) & 31
 
 
 def low_of(word):
@@ -95,7 +101,8 @@
     low = jnp.where(offsets == tiles * LANES, LANES, offsets & (LANES - 1))
     keep = jnp.where((low + numbers >= LANES) & (tile + 1 < tiles), 0, low)
     turn = (low - starts) & (LANES - 1)
-    word = turn + (low << 7) + (keep << 15) + (tile << 23)
+    later = jnp.minimum(tile + 1, tiles - 1)
+    word = turn | (low << 7) | (keep << 15) | (tile << 23) | (later << 28)
     word = jnp.concatenate([word, jnp.zeros((LANES - rows, LANES), jnp.int32)], 0)
     table_ref[...] = word.T[:table_ref.shape[0]]
     rank_ref[...] = rank.astype(jnp.int32)
@@ -141,7 +148,7 @@
             new = []
             for i in range(count):
                 word = table_smem[first + i, j]
-                low, keep, turn, at = low_of(word), keep_of(word), word & (LANES - 1), tile_at(word >> 23)
+                low, keep, turn, at = low_of(word), keep_of(word), word & (LANES - 1), tile_at(tile_of(word))
                 for n, r in enumerate(parts):
                     turned = pltpu.roll(values[n], turn, 1)
                     out = refs[1].at[first + i] if targets > DIRECT else outs[i]
@@ -155,7 +162,7 @@
             out = refs[1].at[first + i] if targets > DIRECT else outs[i]
             word = table_smem[first + i, blocks]
             for n, r in enumerate(parts):
-                out[r:r + ROWS, tile_at(word >> 23)] = jnp.where(lane < low_of(word), held[i * len(parts) + n], 0.0)
+                out[r:r + ROWS, tile_at(tile_of(word))] = jnp.where(lane < low_of(word), held[i * len(parts) + n], 0.0)
 
     if targets <= GROUP:
         place_group(0, targets)
@@ -228,9 +235,8 @@
 
 def increment_part(targets, table_ref, rank_ref, t_ref, slope_ref, refs, out_any, out_ref, sem):
     backs = blocks_of(refs)
-    levels, capacity = backs[0].shape
+    levels, _ = backs[0].shape
     blocks = rank_ref.shape[0]
-    tiles = capacity // LANES
     lane = iota((ROWS, LANES), 1)
     parts = range(0, levels, ROWS)
     me = first_target(targets)
@@ -244,8 +250,7 @@
             found = list(found)
             for i in range(count):
                 word = table_ref[first + i, j]
-                low, tile = low_of(word), word >> 23
-                later = jnp.minimum(tile + 1, tiles - 1)
+                low, tile, later = low_of(word), tile_of(word), lax.shift_right_logical(word, 28)
                 back = refs[0].at[first + i] if targets > DIRECT else backs[i]
                 for n, r in enumerate(parts):
                     window = jnp.where(lane >= low, back[r:r + ROWS, tile_at(tile)], back[r:r + ROWS, tile_at(later)])
@@ -267,21 +272,29 @@
     stores = []
     for p in range(pieces):
         first, last = blocks * p // pieces, blocks * (p + 1) // pieces
-        lax.fori_loop(first, last, block, 0, unroll=4)
+        if targets <= count:
+            for j in range(first, last):
+                block(j, 0)
+        else:
+            lax.fori_loop(first, last, block, 0, unroll=4)
         here = slice(first * LANES, last * LANES)
         stores.append(pltpu.make_async_copy(out_ref.at[:, :, here], out_any.at[:, :, here], sem.at[p]))
         stores[-1].start()
     return lambda: [store.wait() for store in stores]
 
 
-def gate_kernel(targets, group, w_ref, *refs):
+def picked_sources(refs, picks):
+    return [refs[operand] if at is None else refs[operand].at[at] for operand, at in picks]
+
+
+def gate_kernel(targets, group, picks, w_ref, *refs):
     out_any, buffer, picked_ref, sem = refs[-4:]
-    sources = [ref for ref in refs[:-4] if len(ref.shape) == 3]
+    sources = picked_sources(refs, picks)
     gate_part(targets, group, w_ref, sources, out_any, buffer, picked_ref, sem)()
 
 
-def final_kernel(targets, group, columns, backs, table_ref, rank_ref, t_ref, slope_ref, w_ref, *refs):
-    sources, refs = refs[:columns], refs[columns:]
+def final_kernel(targets, group, picks, columns, backs, table_ref, rank_ref, t_ref, slope_ref, w_ref, *refs):
+    sources, refs = picked_sources(refs, picks), refs[columns:]
     returned, refs = refs[:backs], refs[backs:]
     gate_any, out_any, buffer, picked_ref, gate_sem, out_ref, out_sem = refs[-7:]
     gates_done = gate_part(targets, group, w_ref, sources, gate_any, buffer, picked_ref, gate_sem)
@@ -325,7 +338,7 @@
     if direct:
         block_shapes = [shape((level_dev, capacity), f32)] * tile_count
         groups = [range(1, tile_count, 2), range(0, tile_count, 2)]
-        sites = [range(0, half), range(half, tile_count)]
+        sites = [range(0, tile_count, 2), range(1, tile_count, 2)]
     else:
         block_shapes = [shape((tile_count, level_dev, capacity), f32)]
         groups = sites = [range(0, tile_count)]
@@ -370,13 +383,14 @@
             total = total + part
         totals.append(total)
     if direct:
-        incoming = [outgoing[0]]
-        for k in range(1, tile_count):
+        mixed = jnp.concatenate([lax.optimization_barrier(totals[0]), outgoing[1][None]], 0)
+        crossed = exchange(lax.optimization_barrier(mixed), 1)
+        incoming = [outgoing[0], crossed[half]]
+        for k in range(2, tile_count):
             incoming.append(exchange(outgoing[k], k))
         arrived = []
         for site in sites:
-            arrived.append(jnp.stack([incoming[k] for k in site]))
-        crossed = exchange(totals[0], 1)
+            arrived.append(lax.optimization_barrier(jnp.stack([incoming[k] for k in site])))
         restored = []
         for p in range(half):
             pair = jnp.stack([totals[1][p], crossed[p]])
@@ -385,22 +399,32 @@
         arrived = [lax.all_to_all(outgoing[0], "tile", split_axis=0, concat_axis=0, tiled=True)]
         restored = [lax.all_to_all(totals[0], "tile", split_axis=0, concat_axis=0, tiled=True)]
 
+    passed = []
+    for here in arrived:
+        received = []
+        for m in range(1, far):
+            received.append(swap(here, 2 * m))
+        passed.append(received)
+    early = jnp.stack(arrived)
+    early = swap(early, 1)
+    beside = []
+    for received in passed:
+        beside.append([swap(x, 1) for x in received])
+
     gate_values = None
     for n, (group, here) in enumerate(zip(sites, arrived)):
-        columns = [here]
-        for m in range(1, far):
-            columns.append(swap(here, 2 * m))
-        for m in range(far):
-            columns.append(swap(columns[m], 1))
+        final = n + 1 == len(sites)
+        columns = [here] + passed[n] + [early] + beside[n]
+        picks = [(i, None) for i in range(far)] + [(far, n)] + [(far + m, None) for m in range(1, far)]
         before = [] if gate_values is None else [gate_values]
         gate_scratch = [
             pltpu.VMEM((gate_dev, len(group) * capacity), f32),
             pltpu.VMEM(weights.shape[:1] + (gate_dev,), f32),
             pltpu.SemaphoreType.DMA((len(group),)),
         ]
-        if n + 1 < len(sites):
+        if not final:
             gate_values = pl.pallas_call(
-                functools.partial(gate_kernel, tile_count, group),
+                functools.partial(gate_kernel, tile_count, group, picks),
                 out_shape=shape(gate_adjoint.shape, f32),
                 in_specs=[full()] * (1 + len(columns)) + [full(pltpu.HBM)] * len(before),
                 out_specs=full(pltpu.HBM),
@@ -411,7 +435,7 @@
             continue
         operands = [table, rank, t, slopes, weights, *columns, *restored]
         gate_values, increments = pl.pallas_call(
-            functools.partial(final_kernel, tile_count, group, len(columns), len(restored)),
+            functools.partial(final_kernel, tile_count, group, picks, len(columns), len(restored)),
             out_shape=[shape(gate_adjoint.shape, f32), shape(mixing.shape, f32)],
             in_specs=[full(SMEM)] + [full()] * (len(operands) - 1) + [full(pltpu.HBM)] * len(before),
             out_specs=[full(pltpu.HBM)] * 2,

time: 65.7 us -> 59.4 us (0.904)
  starting transfers between devices: 25.3 us -> 20.9 us
  local copies, waits for them, and re-layouts: 1.55 us -> 0.78 us
  Pallas kernels: 12.3 us -> 11.6 us
    ppermute x11 -> x10, starting transfers between devices: 18.7 us -> 15 us  [exchange(): return lax.ppermute(x, 'tile', [(i, i ^ bits) for i in range(tile_count)])]
    unnamed x12, local copies, waits for them, and re-layouts: 1.52 us -> 0.74 us
    pallas_call x2, Pallas kernels: 5.89 us -> 5.14 us  [the longest x1 3.37 us: per_device(): pl.pallas_call(functools.partial(final_kernel, tile_count, group, picks,...]
    ppermute x9 -> x8, starting transfers between devices: 6.54 us -> 5.94 us  [swap(): return lax.ppermute(x, 'lev', [(i, i ^ bits) for i in range(level_count)])]
    ppermute x11 -> x10, waiting for transfers between devices: 14.9 us -> 14.6 us  [exchange(): return lax.ppermute(x, 'tile', [(i, i ^ bits) for i in range(tile_count)])]
    ppermute x9 -> x8, waiting for transfers between devices: 10.5 us -> 10.2 us  [swap(): return lax.ppermute(x, 'lev', [(i, i ^ bits) for i in range(level_count)])]
  transfers between devices with their start and end apart: 20 -> 18, of which waited for: 6 -> 8; matrix products, arithmetic and copies ran while one was open for 0% -> 0% of each run, Pallas kernels for 12% -> 12%
where the time goes in v1:
time: 59.4 us; the launch traced here: 59.1 us
  waiting for transfers between devices  24.8 us (42%)
  starting transfers between devices  20.9 us (35%)
  Pallas kernels  11.6 us (20%)
  between operations  0.82 us (1%)
  local copies, waits for them, and re-layouts  0.78 us (1%)
    ppermute x10, starting transfers between devices, exchange(): return lax.ppermute(x, 'tile', [(i, i ^ bits) for i in range(tile_count)])  15 us
    ppermute x10, waiting for transfers between devices, exchange(): return lax.ppermute(x, 'tile', [(i, i ^ bits) for i in range(tile_count)])  14.6 us
    ppermute x8, waiting for transfers between devices, swap(): return lax.ppermute(x, 'lev', [(i, i ^ bits) for i in range(level_count)])  10.2 us
    ppermute x8, starting transfers between devices, swap(): return lax.ppermute(x, 'lev', [(i, i ^ bits) for i in range(level_count)])  5.94 us
    pallas_call x1, Pallas kernels, per_device(): pl.pallas_call(functools.partial(source_kernel, tile_count), out_shape=[s...  3.82 us
    pallas_call x1, Pallas kernels, per_device(): pl.pallas_call(functools.partial(final_kernel, tile_count, group, picks,...  3.37 us
    pallas_call x2, Pallas kernels, per_device(): pl.pallas_call(functools.partial(adjoint_kernel, tile_count, group), out_...  2.19 us
    pallas_call x1, Pallas kernels, per_device(): pl.pallas_call(functools.partial(gate_kernel, tile_count, group, picks),...  1.77 us
  transfers between devices with their start and end apart: 18, of which 8 were waited for; matrix products, arithmetic and copies ran while one was open for 0% of the time, Pallas kernels for 12%

profile of v1, /device:TPU:0, one launch (start us, length us, event | category | flops | bytes accessed | tf_op | source)
XLA Modules:
  0.0 59.1 jit_solution(5824738931612877283)
XLA Ops:
  0.6 0.6 collective-permute-start
  1.2 0.0 copy-start.4
  1.2 0.7 %copy-done.4 = s32[4096,1]{0,1:T(1,128)S(1)} copy-done((s32[4096,1]{0,1:T(1,128)S(1)}, s32[4096,1]{0,1:T(1,128)}, u32[]{:S(2)}) %copy-start.4) | copy-done | bytes 16408
  1.9 0.0 copy-start
  1.9 0.0 copy-start.3
  1.9 0.4 shard_map.68
  2.3 2.1 %collective-permute-done.near_ref = f32[42,8192]{1,0:T(8,128)S(1)} collective-permute-done((f32[42,8192]{1,0:T(8,128)}, f32[42,8192]{1,0:T(8,128)S(1)}, u32[]{:S(2)}, u32[]{:S(2)}) %collective-permute-start) | collective-permute-done | bytes 1376288 | tf_op jit(solution)/shard_map/ppermute | solution.py:329
  4.4 0.0 copy-done
  4.4 0.0 copy-done.3
  4.4 0.0 copy-start.1
  4.4 0.0 copy-start.2
  4.4 1.1 %shard_map.70 = (f32[4,16,1024]{2,1,0:T(8,128)S(1)}, f32[4,16,1024]{2,1,0:T(8,128)S(1)}) custom-call(f32[64,168]{1,0:T(8,128)S(1)} %bitcast.18, f32[42,8192]{1,0:T(8,128)S(1)} %copy-done, f32[42,8192]{1,0:T(8,128)S(1)} %collective-permute-done.near_ref), custom_call_target="tpu_custom_call" | custom-call | flops 2000000000 | tf_op jit(solution)/shard_map/pallas_call | solution.py:369
  5.6 3.0 %collective-permute-start.1 = (f32[4,16,1024]{2,1,0:T(8,128)S(1)}, f32[4,16,1024]{2,1,0:T(8,128)S(1)}, u32[]{:S(2)}, u32[]{:S(2)}) collective-permute-start(f32[4,16,1024]{2,1,0:T(8,128)S(1)} %get-tuple-element.23), channel_id=1, source_target_pairs={{0,2},{1,3},{2,0},{3,1},{4,6},{5,7},{6,4},{7,5},{8,10},{9,11},{10,... | collective-permute-start | bytes 786440 | tf_op jit(solution)/shard_map/ppermute | solution.py:329
  8.6 0.0 copy-done.1
  8.6 0.0 copy-done.2
  8.6 3.8 %shard_map.69 = (f32[3,16,4096]{2,1,0:T(8,128)S(1)}, f32[16,1024]{1,0:T(8,128)S(1)}, f32[16,1024]{1,0:T(8,128)S(1)}, f32[16,1024]{1,0:T(8,128)S(1)}, f32[16,1024...) custom-call(s32[8,128]{1,0:T(8,128)S(1)} %get-tuple-element.18.table, ...), custom_call_target="tpu_custom_call" | custom-call | flops 4000000000 | tf_op jit(solution)/shard_map/pallas_call | solution.py:354
  12.4 1.6 %collective-permute-start.7 = (f32[16,1024]{1,0:T(8,128)S(1)}, f32[16,1024]{1,0:T(8,128)S(1)}, u32[]{:S(2)}, u32[]{:S(2)}) collective-permute-start(f32[16,1024]{1,0:T(8,128)S(1)} %get-tuple-element.29), channel_id=1, source_target_pairs={{0,8},{4,12},{8,0},{12,4},{16,24},{20,28},{24,16},{28,20},{1,9},{5... | collective-permute-start | bytes 196616 | tf_op jit(solution)/shard_map/ppermute | solution.py:332
  14.1 2.6 %collective-permute-start.8 = (f32[16,1024]{1,0:T(8,128)S(1)}, f32[16,1024]{1,0:T(8,128)S(1)}, u32[]{:S(2)}, u32[]{:S(2)}) collective-permute-start(f32[16,1024]{1,0:T(8,128)S(1)} %get-tuple-element.30), channel_id=1, source_target_pairs={{0,16},{4,20},{8,24},{12,28},{16,0},{20,4},{24,8},{28,12},{1,17},{... | collective-permute-start | bytes 196616 | tf_op jit(solution)/shard_map/ppermute | solution.py:332
  16.6 0.2 collective-permute-start.9
  16.9 0.0 collective-permute-done.7
  16.9 4.5 %collective-permute-done.8 = f32[16,1024]{1,0:T(8,128)S(1)} collective-permute-done((f32[16,1024]{1,0:T(8,128)S(1)}, f32[16,1024]{1,0:T(8,128)S(1)}, u32[]{:S(2)}, u32[]{:S(2)}) %collective-permute-start.8) | collective-permute-done | bytes 65568 | tf_op jit(solution)/shard_map/ppermute | solution.py:332
  21.3 1.4 %collective-permute-done.9 = f32[16,1024]{1,0:T(8,128)S(1)} collective-permute-done((f32[16,1024]{1,0:T(8,128)S(1)}, f32[16,1024]{1,0:T(8,128)S(1)}, u32[]{:S(2)}, u32[]{:S(2)}) %collective-permute-start.9) | collective-permute-done | bytes 65568 | tf_op jit(solution)/shard_map/ppermute | solution.py:332
  22.8 0.5 collective-permute-start.16
  23.3 0.0 collective-permute-done.1
  23.3 1.6 %collective-permute-start.2 = (f32[5,16,1024]{2,1,0:T(8,128)S(1)}, f32[5,16,1024]{2,1,0:T(8,128)S(1)}, u32[]{:S(2)}, u32[]{:S(2)}) collective-permute-start(f32[5,16,1024]{2,1,0:T(8,128)S(1)} %pad_maximum_fusion.1), channel_id=1, source_target_pairs={{0,4},{4,0},{8,12},{12,8},{16,20},{20,16},{24,28},{28,24},{1,5},{5... | collective-permute-start | bytes 983048 | tf_op jit(solution)/shard_map/ppermute | solution.py:332
  24.9 1.1 %shard_map.71 = (f32[4,16,1024]{2,1,0:T(8,128)S(1)}, f32[4,16,1024]{2,1,0:T(8,128)S(1)}) custom-call(f32[64,168]{1,0:T(8,128)S(1)} %bitcast.19, f32[42,8192]{1,0:T(8,128)S(1)} %copy-done, f32[42,8192]{1,0:T(8,128)S(1)} %collective-permute-done.near_ref), custom_call_target="tpu_custom_call" | custom-call | flops 2000000000 | tf_op jit(solution)/shard_map/pallas_call | solution.py:369
  26.0 1.7 %collective-permute-start.12 = (f32[4,16,1024]{2,1,0:T(8,128)S(1)}, f32[4,16,1024]{2,1,0:T(8,128)S(1)}, u32[]{:S(2)}, u32[]{:S(2)}) collective-permute-start(f32[4,16,1024]{2,1,0:T(8,128)S(1)} %get-tuple-element.33), channel_id=1, source_target_pairs={{0,2},{1,3},{2,0},{3,1},{4,6},{5,7},{6,4},{7,5},{8,10},{9,11},{10,... | collective-permute-start | bytes 786440 | tf_op jit(solution)/shard_map/ppermute | solution.py:329
  27.7 0.0 collective-permute-start.3
  27.7 3.2 %collective-permute-start.4 = (f32[16,1024]{1,0:T(8,128)S(1)}, f32[16,1024]{1,0:T(8,128)S(1)}, u32[]{:S(2)}, u32[]{:S(2)}) collective-permute-start(f32[16,1024]{1,0:T(8,128)S(1)} %get-tuple-element.26), channel_id=1, source_target_pairs={{0,20},{4,16},{8,28},{12,24},{16,4},{20,0},{24,12},{28,8},{1,21},{... | collective-permute-start | bytes 196616 | tf_op jit(solution)/shard_map/ppermute | solution.py:332
  30.9 1.1 %collective-permute-done.16.refs_1_ = f32[4,16,1024]{2,1,0:T(8,128)S(1)} collective-permute-done((f32[4,16,1024]{2,1,0:T(8,128)S(1)}, f32[4,16,1024]{2,1,0:T(8,128)S(1)}, u32[]{:S(2)}, u32[]{:S(2)}) %collective-permute-start.16) | collective-permute-done | bytes 262176 | tf_op jit(solution)/shard_map/ppermute | solution.py:329
  32.0 2.0 %collective-permute-start.5 = (f32[16,1024]{1,0:T(8,128)S(1)}, f32[16,1024]{1,0:T(8,128)S(1)}, u32[]{:S(2)}, u32[]{:S(2)}) collective-permute-start(f32[16,1024]{1,0:T(8,128)S(1)} %get-tuple-element.27), channel_id=1, source_target_pairs={{0,28},{4,24},{8,20},{12,16},{16,12},{20,8},{24,4},{28,0},{1,29},{... | collective-permute-start | bytes 196616 | tf_op jit(solution)/shard_map/ppermute | solution.py:332
  34.0 0.8 %collective-permute-done.12 = f32[4,16,1024]{2,1,0:T(8,128)S(1)} collective-permute-done((f32[4,16,1024]{2,1,0:T(8,128)S(1)}, f32[4,16,1024]{2,1,0:T(8,128)S(1)}, u32[]{:S(2)}, u32[]{:S(2)}) %collective-permute-start.12) | collective-permute-done | bytes 262176 | tf_op jit(solution)/shard_map/ppermute | solution.py:329
  34.9 0.0 collective-permute-start.17
  34.9 0.0 collective-permute-done.2
  34.9 0.0 collective-permute-done.3
  35.0 0.0 collective-permute-done.4
  35.0 4.0 %collective-permute-done.5 = f32[16,1024]{1,0:T(8,128)S(1)} collective-permute-done((f32[16,1024]{1,0:T(8,128)S(1)}, f32[16,1024]{1,0:T(8,128)S(1)}, u32[]{:S(2)}, u32[]{:S(2)}) %collective-permute-start.5) | collective-permute-done | bytes 65568 | tf_op jit(solution)/shard_map/ppermute | solution.py:332
  39.0 0.1 pad_maximum_fusion
  39.0 0.1 collective-permute-start.10
  39.2 0.1 collective-permute-start.6
  39.3 0.1 collective-permute-start.13
  39.4 2.4 %collective-permute-start.14 = (f32[2,16,1024]{2,1,0:T(8,128)S(1)}, f32[2,16,1024]{2,1,0:T(8,128)S(1)}, u32[]{:S(2)}, u32[]{:S(2)}) collective-permute-start(f32[2,16,1024]{2,1,0:T(8,128)S(1)} %pad_maximum_fusion.6), channel_id=1, source_target_pairs={{0,16},{4,20},{8,24},{12,28},{16,0},{20,4},{24,8},{28,12},{1,17},{... | collective-permute-start | bytes 393224 | tf_op jit(solution)/shard_map/ppermute | solution.py:332
  41.8 6.2 %collective-permute-done.6.refs_1_ = f32[4,16,1024]{2,1,0:T(8,128)S(1)} collective-permute-done((f32[4,16,1024]{2,1,0:T(8,128)S(1)}, f32[4,16,1024]{2,1,0:T(8,128)S(1)}, u32[]{:S(2)}, u32[]{:S(2)}) %collective-permute-start.6) | collective-permute-done | bytes 262176 | tf_op jit(solution)/shard_map/ppermute | solution.py:329
  47.9 0.0 collective-permute-start.11
  47.9 0.0 copy-start.5
  48.0 0.0 collective-permute-done.17.refs_3_
  48.0 1.3 %collective-permute-start.15 = (f32[2,16,1024]{2,1,0:T(8,128)S(1)}, f32[2,16,1024]{2,1,0:T(8,128)S(1)}, u32[]{:S(2)}, u32[]{:S(2)}) collective-permute-start(f32[2,16,1024]{2,1,0:T(8,128)S(1)} %pad_maximum_fusion.7), channel_id=1, source_target_pairs={{0,24},{4,28},{8,16},{12,20},{16,8},{20,12},{24,0},{28,4},{1,25},{... | collective-permute-start | bytes 393224 | tf_op jit(solution)/shard_map/ppermute | solution.py:332
  49.2 0.0 collective-permute-done.10.refs_2_
  49.2 1.8 %shard_map.72.refs_8_ = f32[42,8192]{1,0:T(8,128)} custom-call(f32[64,168]{1,0:T(8,128)S(1)} %bitcast.20, f32[4,16,1024]{2,1,0:T(8,128)S(1)} %pad_maximum_fusion.3.refs_0_, f32[4,16,1024]{2,1,0:T(8,128)S(1)} %collective-permute-done.16.refs_1_, f32[2,4,16,1024]{3,2,1,0:T(8,128)S(1)} %collective-permute-done.10.refs_2_, ...), custom_call_target="tpu_custom_call" | custom-call | flops 2000000000 | tf_op jit(solution)/shard_map/pallas_call | solution.py:426
  51.0 0.0 collective-permute-done.13.refs_5_
  51.0 0.0 collective-permute-done.14.refs_6_
  51.0 4.7 %collective-permute-done.15.refs_7_ = f32[2,16,1024]{2,1,0:T(8,128)S(1)} collective-permute-done((f32[2,16,1024]{2,1,0:T(8,128)S(1)}, f32[2,16,1024]{2,1,0:T(8,128)S(1)}, u32[]{:S(2)}, u32[]{:S(2)}) %collective-permute-start.15) | collective-permute-done | bytes 131104 | tf_op jit(solution)/shard_map/ppermute | solution.py:332
  55.7 0.0 collective-permute-done.11.refs_3_
  55.7 0.0 copy-done.5
  55.7 3.4 %shard_map.73 = (f32[42,8192]{1,0:T(8,128)}, f32[3,16,4096]{2,1,0:T(8,128)}) custom-call(s32[8,128]{1,0:T(8,128)S(1)} %get-tuple-element.18.table_ref, s32[32,128]{1,0:T(8,128)S(1)} %get-tuple-element.19.rank_ref, s32[32,128]{1,0:T(8,128)S(1)} %bitcast.23, f32[3,16,4096]{2,1,0:T(8,128)S(1)} %get-tuple-element.21.slope_ref, ...), custom_call_target="tpu_custom_call", output_to_operand_aliasing={{0}: (13, {})} | custom-call | flops 4000000000 | tf_op jit(solution)/shard_map/pallas_call | solution.py:437
  (11 shorter events, 0.2 us)
Async XLA Ops:
  0.6 3.8 %collective-permute-start = (f32[42,8192]{1,0:T(8,128)}, f32[42,8192]{1,0:T(8,128)S(1)}, u32[]{:S(2)}, u32[]{:S(2)}) collective-permute-start(f32[42,8192]{1,0:T(8,128)} %own_ref.3), channel_id=1, source_target_pairs={{0,1},{1,0},{2,3},{3,2},{4,5},{5,4},{6,7},{7,6},{8,9},{9,8},{10,11... | collective-permute-start | bytes 4128776 | tf_op jit(solution)/shard_map/ppermute | solution.py:329
  1.2 0.7 %copy-start.4 = (s32[4096,1]{0,1:T(1,128)S(1)}, s32[4096,1]{0,1:T(1,128)}, u32[]{:S(2)}) copy-start(s32[4096,1]{0,1:T(1,128)} %param.7) | copy-start | bytes 49156
  1.9 2.5 %copy-start = (f32[42,8192]{1,0:T(8,128)S(1)}, f32[42,8192]{1,0:T(8,128)}, u32[]{:S(2)}) copy-start(f32[42,8192]{1,0:T(8,128)} %own_ref.3) | copy-start | bytes 4128772
  1.9 2.5 %copy-start.3 = (f32[1,168,64]{1,2,0:T(8,128)S(1)}, f32[1,168,64]{1,2,0:T(8,128)}, u32[]{:S(2)}) copy-start(f32[1,168,64]{1,2,0:T(8,128)} %param.8) | copy-start | bytes 129028
  4.4 4.1 %copy-start.1 = (f32[3,16,4096]{2,1,0:T(8,128)S(1)}, f32[3,16,4096]{2,1,0:T(8,128)}, u32[]{:S(2)}) copy-start(f32[3,16,4096]{2,1,0:T(8,128)} %mixing_ref.1) | copy-start | bytes 2359300
  4.4 4.1 %copy-start.2 = (f32[16,4096]{1,0:T(8,128)S(1)}, f32[16,4096]{1,0:T(8,128)}, u32[]{:S(2)}) copy-start(f32[16,4096]{1,0:T(8,128)} %density_ref.1) | copy-start | bytes 786436
  5.6 17.7 %collective-permute-start.1 = (f32[4,16,1024]{2,1,0:T(8,128)S(1)}, f32[4,16,1024]{2,1,0:T(8,128)S(1)}, u32[]{:S(2)}, u32[]{:S(2)}) collective-permute-start(f32[4,16,1024]{2,1,0:T(8,128)S(1)} %get-tuple-element.23), channel_id=1, source_target_pairs={{0,2},{1,3},{2,0},{3,1},{4,6},{5,7},{6,4},{7,5},{8,10},{9,11},{10,... | collective-permute-start | bytes 786440 | tf_op jit(solution)/shard_map/ppermute | solution.py:329
  12.4 4.5 %collective-permute-start.7 = (f32[16,1024]{1,0:T(8,128)S(1)}, f32[16,1024]{1,0:T(8,128)S(1)}, u32[]{:S(2)}, u32[]{:S(2)}) collective-permute-start(f32[16,1024]{1,0:T(8,128)S(1)} %get-tuple-element.29), channel_id=1, source_target_pairs={{0,8},{4,12},{8,0},{12,4},{16,24},{20,28},{24,16},{28,20},{1,9},{5... | collective-permute-start | bytes 196616 | tf_op jit(solution)/shard_map/ppermute | solution.py:332
  14.1 7.3 %collective-permute-start.8 = (f32[16,1024]{1,0:T(8,128)S(1)}, f32[16,1024]{1,0:T(8,128)S(1)}, u32[]{:S(2)}, u32[]{:S(2)}) collective-permute-start(f32[16,1024]{1,0:T(8,128)S(1)} %get-tuple-element.30), channel_id=1, source_target_pairs={{0,16},{4,20},{8,24},{12,28},{16,0},{20,4},{24,8},{28,12},{1,17},{... | collective-permute-start | bytes 196616 | tf_op jit(solution)/shard_map/ppermute | solution.py:332
  16.6 6.1 %collective-permute-start.9 = (f32[16,1024]{1,0:T(8,128)S(1)}, f32[16,1024]{1,0:T(8,128)S(1)}, u32[]{:S(2)}, u32[]{:S(2)}) collective-permute-start(f32[16,1024]{1,0:T(8,128)S(1)} %get-tuple-element.31), channel_id=1, source_target_pairs={{0,24},{4,28},{8,16},{12,20},{16,8},{20,12},{24,0},{28,4},{1,25},{... | collective-permute-start | bytes 196616 | tf_op jit(solution)/shard_map/ppermute | solution.py:332
  22.8 9.2 %collective-permute-start.16 = (f32[4,16,1024]{2,1,0:T(8,128)S(1)}, f32[4,16,1024]{2,1,0:T(8,128)S(1)}, u32[]{:S(2)}, u32[]{:S(2)}) collective-permute-start(f32[4,16,1024]{2,1,0:T(8,128)S(1)} %pad_maximum_fusion.3.refs_0_), channel_id=1, source_target_pairs={{0,2},{1,3},{2,0},{3,1},{4,6},{5,7},{6,4},{7,5},{8,10},{9,11},{10,... | collective-permute-start | bytes 786440 | tf_op jit(solution)/shard_map/ppermute | solution.py:329
  23.3 11.6 %collective-permute-start.2 = (f32[5,16,1024]{2,1,0:T(8,128)S(1)}, f32[5,16,1024]{2,1,0:T(8,128)S(1)}, u32[]{:S(2)}, u32[]{:S(2)}) collective-permute-start(f32[5,16,1024]{2,1,0:T(8,128)S(1)} %pad_maximum_fusion.1), channel_id=1, source_target_pairs={{0,4},{4,0},{8,12},{12,8},{16,20},{20,16},{24,28},{28,24},{1,5},{5... | collective-permute-start | bytes 983048 | tf_op jit(solution)/shard_map/ppermute | solution.py:332
  26.0 8.9 %collective-permute-start.12 = (f32[4,16,1024]{2,1,0:T(8,128)S(1)}, f32[4,16,1024]{2,1,0:T(8,128)S(1)}, u32[]{:S(2)}, u32[]{:S(2)}) collective-permute-start(f32[4,16,1024]{2,1,0:T(8,128)S(1)} %get-tuple-element.33), channel_id=1, source_target_pairs={{0,2},{1,3},{2,0},{3,1},{4,6},{5,7},{6,4},{7,5},{8,10},{9,11},{10,... | collective-permute-start | bytes 786440 | tf_op jit(solution)/shard_map/ppermute | solution.py:329
  27.7 7.2 %collective-permute-start.3 = (f32[16,1024]{1,0:T(8,128)S(1)}, f32[16,1024]{1,0:T(8,128)S(1)}, u32[]{:S(2)}, u32[]{:S(2)}) collective-permute-start(f32[16,1024]{1,0:T(8,128)S(1)} %get-tuple-element.25), channel_id=1, source_target_pairs={{0,12},{4,8},{8,4},{12,0},{16,28},{20,24},{24,20},{28,16},{1,13},{... | collective-permute-start | bytes 196616 | tf_op jit(solution)/shard_map/ppermute | solution.py:332
  27.7 7.3 %collective-permute-start.4 = (f32[16,1024]{1,0:T(8,128)S(1)}, f32[16,1024]{1,0:T(8,128)S(1)}, u32[]{:S(2)}, u32[]{:S(2)}) collective-permute-start(f32[16,1024]{1,0:T(8,128)S(1)} %get-tuple-element.26), channel_id=1, source_target_pairs={{0,20},{4,16},{8,28},{12,24},{16,4},{20,0},{24,12},{28,8},{1,21},{... | collective-permute-start | bytes 196616 | tf_op jit(solution)/shard_map/ppermute | solution.py:332
  32.0 7.0 %collective-permute-start.5 = (f32[16,1024]{1,0:T(8,128)S(1)}, f32[16,1024]{1,0:T(8,128)S(1)}, u32[]{:S(2)}, u32[]{:S(2)}) collective-permute-start(f32[16,1024]{1,0:T(8,128)S(1)} %get-tuple-element.27), channel_id=1, source_target_pairs={{0,28},{4,24},{8,20},{12,16},{16,12},{20,8},{24,4},{28,0},{1,29},{... | collective-permute-start | bytes 196616 | tf_op jit(solution)/shard_map/ppermute | solution.py:332
  34.9 13.1 %collective-permute-start.17 = (f32[4,16,1024]{2,1,0:T(8,128)S(1)}, f32[4,16,1024]{2,1,0:T(8,128)S(1)}, u32[]{:S(2)}, u32[]{:S(2)}) collective-permute-start(f32[4,16,1024]{2,1,0:T(8,128)S(1)} %collective-permute-done.16.refs_1_), channel_id=1, source_target_pairs={{0,1},{1,0},{2,3},{3,2},{4,5},{5,4},{6,7},{7,6},{8,9},{9,8},{10,11... | collective-permute-start | bytes 786440 | tf_op jit(solution)/shard_map/ppermute | solution.py:329
  39.0 10.2 %collective-permute-start.10 = (f32[2,4,16,1024]{3,2,1,0:T(8,128)S(1)}, f32[2,4,16,1024]{3,2,1,0:T(8,128)S(1)}, u32[]{:S(2)}, u32[]{:S(2)}) collective-permute-start(f32[2,4,16,1024]{3,2,1,0:T(8,128)S(1)} %pad_maximum_fusion), channel_id=1, source_target_pairs={{0,1},{1,0},{2,3},{3,2},{4,5},{5,4},{6,7},{7,6},{8,9},{9,8},{10,11... | collective-permute-start | bytes 1572872 | tf_op jit(solution)/shard_map/ppermute | solution.py:329
  39.2 8.8 %collective-permute-start.6 = (f32[4,16,1024]{2,1,0:T(8,128)S(1)}, f32[4,16,1024]{2,1,0:T(8,128)S(1)}, u32[]{:S(2)}, u32[]{:S(2)}) collective-permute-start(f32[4,16,1024]{2,1,0:T(8,128)S(1)} %pad_maximum_fusion.2.refs_0_), channel_id=1, source_target_pairs={{0,2},{1,3},{2,0},{3,1},{4,6},{5,7},{6,4},{7,5},{8,10},{9,11},{10,... | collective-permute-start | bytes 786440 | tf_op jit(solution)/shard_map/ppermute | solution.py:329
  39.3 11.7 %collective-permute-start.13 = (f32[2,16,1024]{2,1,0:T(8,128)S(1)}, f32[2,16,1024]{2,1,0:T(8,128)S(1)}, u32[]{:S(2)}, u32[]{:S(2)}) collective-permute-start(f32[2,16,1024]{2,1,0:T(8,128)S(1)} %pad_maximum_fusion.5), channel_id=1, source_target_pairs={{0,8},{4,12},{8,0},{12,4},{16,24},{20,28},{24,16},{28,20},{1,9},{5... | collective-permute-start | bytes 393224 | tf_op jit(solution)/shard_map/ppermute | solution.py:332
  39.4 11.7 %collective-permute-start.14 = (f32[2,16,1024]{2,1,0:T(8,128)S(1)}, f32[2,16,1024]{2,1,0:T(8,128)S(1)}, u32[]{:S(2)}, u32[]{:S(2)}) collective-permute-start(f32[2,16,1024]{2,1,0:T(8,128)S(1)} %pad_maximum_fusion.6), channel_id=1, source_target_pairs={{0,16},{4,20},{8,24},{12,28},{16,0},{20,4},{24,8},{28,12},{1,17},{... | collective-permute-start | bytes 393224 | tf_op jit(solution)/shard_map/ppermute | solution.py:332
  47.9 7.8 %collective-permute-start.11 = (f32[4,16,1024]{2,1,0:T(8,128)S(1)}, f32[4,16,1024]{2,1,0:T(8,128)S(1)}, u32[]{:S(2)}, u32[]{:S(2)}) collective-permute-start(f32[4,16,1024]{2,1,0:T(8,128)S(1)} %collective-permute-done.6.refs_1_), channel_id=1, source_target_pairs={{0,1},{1,0},{2,3},{3,2},{4,5},{5,4},{6,7},{7,6},{8,9},{9,8},{10,11... | collective-permute-start | bytes 786440 | tf_op jit(solution)/shard_map/ppermute | solution.py:329
  47.9 7.8 %copy-start.5 = (s32[4096,1]{0,1:T(1,128)S(1)}, s32[4096,1]{0,1:T(1,128)}, u32[]{:S(2)}) copy-start(s32[4096,1]{0,1:T(1,128)} %param.7) | copy-start | bytes 49156
  48.0 7.8 %collective-permute-start.15 = (f32[2,16,1024]{2,1,0:T(8,128)S(1)}, f32[2,16,1024]{2,1,0:T(8,128)S(1)}, u32[]{:S(2)}, u32[]{:S(2)}) collective-permute-start(f32[2,16,1024]{2,1,0:T(8,128)S(1)} %pad_maximum_fusion.7), channel_id=1, source_target_pairs={{0,24},{4,28},{8,16},{12,20},{16,8},{20,12},{24,0},{28,4},{1,25},{... | collective-permute-start | bytes 393224 | tf_op jit(solution)/shard_map/ppermute | solution.py:332

commit v2 on v1

--- a/solution.py
+++ b/solution.py
@@ -13,7 +13,6 @@
 ROWS = 8
 GROUP = 8
 DIRECT = 8
-SMEM = pltpu.SMEM
 
 
 def iota(shape, dim):
@@ -233,7 +232,8 @@
     return lambda: lax.fori_loop(0, len(group), finish, 0)
 
 
-def increment_part(targets, table_ref, rank_ref, t_ref, slope_ref, refs, out_any, out_ref, sem):
+def increment_kernel(targets, table_ref, rank_ref, t_ref, slope_ref, *refs):
+    refs, out_ref = refs[:-1], refs[-1]
     backs = blocks_of(refs)
     levels, _ = backs[0].shape
     blocks = rank_ref.shape[0]
@@ -268,19 +268,11 @@
                 out_ref[k, r:r + ROWS, tile_at(j)] = slope_ref[k, r:r + ROWS, tile_at(j)] * found[n]
         return carry
 
-    pieces = sem.shape[0]
-    stores = []
-    for p in range(pieces):
-        first, last = blocks * p // pieces, blocks * (p + 1) // pieces
-        if targets <= count:
-            for j in range(first, last):
-                block(j, 0)
-        else:
-            lax.fori_loop(first, last, block, 0, unroll=4)
-        here = slice(first * LANES, last * LANES)
-        stores.append(pltpu.make_async_copy(out_ref.at[:, :, here], out_any.at[:, :, here], sem.at[p]))
-        stores[-1].start()
-    return lambda: [store.wait() for store in stores]
+    if targets <= count:
+        for j in range(blocks):
+            block(j, 0)
+    else:
+        lax.fori_loop(0, blocks, block, 0, unroll=4)
 
 
 def picked_sources(refs, picks):
@@ -293,15 +285,13 @@
     gate_part(targets, group, w_ref, sources, out_any, buffer, picked_ref, sem)()
 
 
-def final_kernel(targets, group, picks, columns, backs, table_ref, rank_ref, t_ref, slope_ref, w_ref, *refs):
-    sources, refs = picked_sources(refs, picks), refs[columns:]
-    returned, refs = refs[:backs], refs[backs:]
-    gate_any, out_any, buffer, picked_ref, gate_sem, out_ref, out_sem = refs[-7:]
-    gates_done = gate_part(targets, group, w_ref, sources, gate_any, buffer, picked_ref, gate_sem)
-    increments_done = increment_part(
-        targets, table_ref, rank_ref, t_ref, slope_ref, returned, out_any, out_ref, out_sem)
-    gates_done()
-    increments_done()
+def final_kernel(targets, group, picks, columns, increment_ref, w_ref, *refs):
+    sources = picked_sources(refs[:columns], picks)
+    gate_any, out_any, buffer, picked_ref, gate_sem, out_sem = refs[-6:]
+    store = pltpu.make_async_copy(increment_ref, out_any, out_sem)
+    store.start()
+    gate_part(targets, group, w_ref, sources, gate_any, buffer, picked_ref, gate_sem)()
+    store.wait()
 
 
 def settings(mib, micros):
@@ -405,17 +395,19 @@
         for m in range(1, far):
             received.append(swap(here, 2 * m))
         passed.append(received)
-    early = jnp.stack(arrived)
-    early = swap(early, 1)
     beside = []
-    for received in passed:
-        beside.append([swap(x, 1) for x in received])
+    for n, received in enumerate(passed[:-1]):
+        beside.append([swap(arrived[n], 1)])
+        beside[n] += [swap(x, 1) for x in received]
+    late = jnp.stack([arrived[-1]] + passed[-1])
+    beside.append([swap(late, 1)])
 
     gate_values = None
     for n, (group, here) in enumerate(zip(sites, arrived)):
         final = n + 1 == len(sites)
-        columns = [here] + passed[n] + [early] + beside[n]
-        picks = [(i, None) for i in range(far)] + [(far, n)] + [(far + m, None) for m in range(1, far)]
+        columns = [here] + passed[n] + beside[n]
+        picks = [(i, None) for i in range(far)]
+        picks += [(far, m) if final else (far + m, None) for m in range(far)]
         before = [] if gate_values is None else [gate_values]
         gate_scratch = [
             pltpu.VMEM((gate_dev, len(group) * capacity), f32),
@@ -433,15 +425,22 @@
                 **settings(12, 2),
             )(weights, *columns, *before)
             continue
-        operands = [table, rank, t, slopes, weights, *columns, *restored]
+        found = pl.pallas_call(
+            functools.partial(increment_kernel, tile_count),
+            out_shape=shape(mixing.shape, f32),
+            in_specs=[full(pltpu.SMEM)] + [full()] * (3 + len(restored)),
+            out_specs=full(),
+            **settings(12, 1),
+        )(table, rank, t, slopes, *restored)
+        operands = [found, weights, *columns]
         gate_values, increments = pl.pallas_call(
-            functools.partial(final_kernel, tile_count, group, picks, len(columns), len(restored)),
+            functools.partial(final_kernel, tile_count, group, picks, len(columns)),
             out_shape=[shape(gate_adjoint.shape, f32), shape(mixing.shape, f32)],
-            in_specs=[full(SMEM)] + [full()] * (len(operands) - 1) + [full(pltpu.HBM)] * len(before),
+            in_specs=[full()] * len(operands) + [full(pltpu.HBM)] * len(before),
             out_specs=[full(pltpu.HBM)] * 2,
             input_output_aliases={len(operands): 0} if before else {},
-            scratch_shapes=gate_scratch + [pltpu.VMEM(mixing.shape, f32), pltpu.SemaphoreType.DMA((4,))],
-            **settings(16, 4),
+            scratch_shapes=gate_scratch + [pltpu.SemaphoreType.DMA],
+            **settings(16, 2),
         )(*operands, *before)
     return gate_values, increments
 

time: 59.4 us -> 57.5 us (0.968)
  waiting for transfers between devices: 24.8 us -> 19.5 us
  starting transfers between devices: 20.9 us -> 24.4 us
    ppermute x10, starting transfers between devices: 15 us -> 18.2 us  [exchange(): return lax.ppermute(x, 'tile', [(i, i ^ bits) for i in range(tile_count)])]
    ppermute x10, waiting for transfers between devices: 14.6 us -> 11.7 us  [exchange(): return lax.ppermute(x, 'tile', [(i, i ^ bits) for i in range(tile_count)])]
    ppermute x8, waiting for transfers between devices: 10.2 us -> 7.79 us  [swap(): return lax.ppermute(x, 'lev', [(i, i ^ bits) for i in range(level_count)])]
    pallas_call x1, Pallas kernels: 3.37 us -> 1.8 us  [per_device(): pl.pallas_call(functools.partial(final_kernel, tile_count, group, picks,...]
    pallas_call x0 -> x1, Pallas kernels: none -> 1.56 us  [per_device(): pl.pallas_call(functools.partial(increment_kernel, tile_count), out_shape...]
  transfers between devices with their start and end apart: 18 -> 18, of which waited for: 8 -> 7; matrix products, arithmetic and copies ran while one was open for 0% -> 0% of each run, Pallas kernels for 12% -> 15%
where the time goes in v2:
time: 57.5 us; the launch traced here: 57.3 us
  starting transfers between devices  24.4 us (42%)
  waiting for transfers between devices  19.5 us (34%)
  Pallas kernels  11.5 us (20%)
  between operations  0.83 us (1%)
  local copies, waits for them, and re-layouts  0.78 us (1%)
    ppermute x10, starting transfers between devices, exchange(): return lax.ppermute(x, 'tile', [(i, i ^ bits) for i in range(tile_count)])  18.2 us
    ppermute x10, waiting for transfers between devices, exchange(): return lax.ppermute(x, 'tile', [(i, i ^ bits) for i in range(tile_count)])  11.7 us
    ppermute x8, waiting for transfers between devices, swap(): return lax.ppermute(x, 'lev', [(i, i ^ bits) for i in range(level_count)])  7.79 us
    ppermute x8, starting transfers between devices, swap(): return lax.ppermute(x, 'lev', [(i, i ^ bits) for i in range(level_count)])  6.21 us
    pallas_call x1, Pallas kernels, per_device(): pl.pallas_call(functools.partial(source_kernel, tile_count), out_shape=[s...  3.82 us
    pallas_call x2, Pallas kernels, per_device(): pl.pallas_call(functools.partial(adjoint_kernel, tile_count, group), out_...  2.18 us
    pallas_call x1, Pallas kernels, per_device(): pl.pallas_call(functools.partial(final_kernel, tile_count, group, picks,...  1.8 us
    pallas_call x1, Pallas kernels, per_device(): pl.pallas_call(functools.partial(gate_kernel, tile_count, group, picks),...  1.77 us
  transfers between devices with their start and end apart: 18, of which 7 were waited for; matrix products, arithmetic and copies ran while one was open for 0% of the time, Pallas kernels for 15%

profile of v2, /device:TPU:0, one launch (start us, length us, event | category | flops | bytes accessed | tf_op | source)
XLA Modules:
  0.0 57.3 jit_solution(8356843367093404823)
XLA Ops:
  0.6 0.6 collective-permute-start
  1.2 0.0 copy-start.4
  1.2 0.7 %copy-done.4 = s32[4096,1]{0,1:T(1,128)S(1)} copy-done((s32[4096,1]{0,1:T(1,128)S(1)}, s32[4096,1]{0,1:T(1,128)}, u32[]{:S(2)}) %copy-start.4) | copy-done | bytes 16408
  1.9 0.0 copy-start
  1.9 0.0 copy-start.3
  1.9 0.4 shard_map.68
  2.3 2.1 %collective-permute-done.near_ref = f32[42,8192]{1,0:T(8,128)S(1)} collective-permute-done((f32[42,8192]{1,0:T(8,128)}, f32[42,8192]{1,0:T(8,128)S(1)}, u32[]{:S(2)}, u32[]{:S(2)}) %collective-permute-start) | collective-permute-done | bytes 1376288 | tf_op jit(solution)/shard_map/ppermute | solution.py:319
  4.4 0.0 copy-done
  4.4 0.0 copy-done.3
  4.4 0.0 copy-start.1
  4.4 0.0 copy-start.2
  4.4 1.1 %shard_map.71 = (f32[4,16,1024]{2,1,0:T(8,128)S(1)}, f32[4,16,1024]{2,1,0:T(8,128)S(1)}) custom-call(f32[64,168]{1,0:T(8,128)S(1)} %bitcast.18, f32[42,8192]{1,0:T(8,128)S(1)} %copy-done, f32[42,8192]{1,0:T(8,128)S(1)} %collective-permute-done.near_ref), custom_call_target="tpu_custom_call" | custom-call | flops 2000000000 | tf_op jit(solution)/shard_map/pallas_call | solution.py:359
  5.6 3.0 %collective-permute-start.2 = (f32[4,16,1024]{2,1,0:T(8,128)S(1)}, f32[4,16,1024]{2,1,0:T(8,128)S(1)}, u32[]{:S(2)}, u32[]{:S(2)}) collective-permute-start(f32[4,16,1024]{2,1,0:T(8,128)S(1)} %get-tuple-element.25), channel_id=1, source_target_pairs={{0,2},{1,3},{2,0},{3,1},{4,6},{5,7},{6,4},{7,5},{8,10},{9,11},{10,... | collective-permute-start | bytes 786440 | tf_op jit(solution)/shard_map/ppermute | solution.py:319
  8.6 0.0 copy-done.1
  8.6 0.0 copy-done.2
  8.6 3.8 %shard_map.69 = (f32[3,16,4096]{2,1,0:T(8,128)S(1)}, f32[16,1024]{1,0:T(8,128)S(1)}, f32[16,1024]{1,0:T(8,128)S(1)}, f32[16,1024]{1,0:T(8,128)S(1)}, f32[16,1024...) custom-call(s32[8,128]{1,0:T(8,128)S(1)} %get-tuple-element.18.table, ...), custom_call_target="tpu_custom_call" | custom-call | flops 4000000000 | tf_op jit(solution)/shard_map/pallas_call | solution.py:344
  12.4 1.6 %collective-permute-start.12 = (f32[16,1024]{1,0:T(8,128)S(1)}, f32[16,1024]{1,0:T(8,128)S(1)}, u32[]{:S(2)}, u32[]{:S(2)}) collective-permute-start(f32[16,1024]{1,0:T(8,128)S(1)} %get-tuple-element.31), channel_id=1, source_target_pairs={{0,8},{4,12},{8,0},{12,4},{16,24},{20,28},{24,16},{28,20},{1,9},{5... | collective-permute-start | bytes 196616 | tf_op jit(solution)/shard_map/ppermute | solution.py:322
  14.1 2.6 %collective-permute-start.13 = (f32[16,1024]{1,0:T(8,128)S(1)}, f32[16,1024]{1,0:T(8,128)S(1)}, u32[]{:S(2)}, u32[]{:S(2)}) collective-permute-start(f32[16,1024]{1,0:T(8,128)S(1)} %get-tuple-element.32), channel_id=1, source_target_pairs={{0,16},{4,20},{8,24},{12,28},{16,0},{20,4},{24,8},{28,12},{1,17},{... | collective-permute-start | bytes 196616 | tf_op jit(solution)/shard_map/ppermute | solution.py:322
  16.6 0.2 collective-permute-start.14
  16.9 1.1 %shard_map.70 = (f32[4,16,1024]{2,1,0:T(8,128)S(1)}, f32[4,16,1024]{2,1,0:T(8,128)S(1)}) custom-call(f32[64,168]{1,0:T(8,128)S(1)} %bitcast.19, f32[42,8192]{1,0:T(8,128)S(1)} %copy-done, f32[42,8192]{1,0:T(8,128)S(1)} %collective-permute-done.near_ref), custom_call_target="tpu_custom_call" | custom-call | flops 2000000000 | tf_op jit(solution)/shard_map/pallas_call | solution.py:359
  17.9 0.4 collective-permute-start.1
  18.3 0.0 collective-permute-done.2
  18.4 1.8 %collective-permute-start.3 = (f32[5,16,1024]{2,1,0:T(8,128)S(1)}, f32[5,16,1024]{2,1,0:T(8,128)S(1)}, u32[]{:S(2)}, u32[]{:S(2)}) collective-permute-start(f32[5,16,1024]{2,1,0:T(8,128)S(1)} %pad_maximum_fusion.1), channel_id=1, source_target_pairs={{0,4},{4,0},{8,12},{12,8},{16,20},{20,16},{24,28},{28,24},{1,5},{5... | collective-permute-start | bytes 983048 | tf_op jit(solution)/shard_map/ppermute | solution.py:322
  20.2 0.0 collective-permute-done.12
  20.2 1.2 %collective-permute-done.13 = f32[16,1024]{1,0:T(8,128)S(1)} collective-permute-done((f32[16,1024]{1,0:T(8,128)S(1)}, f32[16,1024]{1,0:T(8,128)S(1)}, u32[]{:S(2)}, u32[]{:S(2)}) %collective-permute-start.13) | collective-permute-done | bytes 65568 | tf_op jit(solution)/shard_map/ppermute | solution.py:322
  21.3 1.4 %collective-permute-done.14 = f32[16,1024]{1,0:T(8,128)S(1)} collective-permute-done((f32[16,1024]{1,0:T(8,128)S(1)}, f32[16,1024]{1,0:T(8,128)S(1)}, u32[]{:S(2)}, u32[]{:S(2)}) %collective-permute-start.14) | collective-permute-done | bytes 65568 | tf_op jit(solution)/shard_map/ppermute | solution.py:322
  22.8 0.5 collective-permute-start.15
  23.3 0.8 %collective-permute-start.7 = (f32[16,1024]{1,0:T(8,128)S(1)}, f32[16,1024]{1,0:T(8,128)S(1)}, u32[]{:S(2)}, u32[]{:S(2)}) collective-permute-start(f32[16,1024]{1,0:T(8,128)S(1)} %get-tuple-element.27), channel_id=1, source_target_pairs={{0,12},{4,8},{8,4},{12,0},{16,28},{20,24},{24,20},{28,16},{1,13},{... | collective-permute-start | bytes 196616 | tf_op jit(solution)/shard_map/ppermute | solution.py:322
  24.1 2.8 %collective-permute-start.8 = (f32[16,1024]{1,0:T(8,128)S(1)}, f32[16,1024]{1,0:T(8,128)S(1)}, u32[]{:S(2)}, u32[]{:S(2)}) collective-permute-start(f32[16,1024]{1,0:T(8,128)S(1)} %get-tuple-element.28), channel_id=1, source_target_pairs={{0,20},{4,16},{8,28},{12,24},{16,4},{20,0},{24,12},{28,8},{1,21},{... | collective-permute-start | bytes 196616 | tf_op jit(solution)/shard_map/ppermute | solution.py:322
  26.8 0.1 collective-permute-done.1
  27.0 4.8 %collective-permute-start.9 = (f32[16,1024]{1,0:T(8,128)S(1)}, f32[16,1024]{1,0:T(8,128)S(1)}, u32[]{:S(2)}, u32[]{:S(2)}) collective-permute-start(f32[16,1024]{1,0:T(8,128)S(1)} %get-tuple-element.29), channel_id=1, source_target_pairs={{0,28},{4,24},{8,20},{12,16},{16,12},{20,8},{24,4},{28,0},{1,29},{... | collective-permute-start | bytes 196616 | tf_op jit(solution)/shard_map/ppermute | solution.py:322
  31.8 0.0 collective-permute-done.15.refs_1_
  31.8 0.1 collective-permute-start.16
  31.8 0.0 collective-permute-done.3
  31.9 0.5 collective-permute-start.17
  32.4 0.0 collective-permute-done.7
  32.4 0.0 collective-permute-done.8
  32.4 1.6 %collective-permute-done.9 = f32[16,1024]{1,0:T(8,128)S(1)} collective-permute-done((f32[16,1024]{1,0:T(8,128)S(1)}, f32[16,1024]{1,0:T(8,128)S(1)}, u32[]{:S(2)}, u32[]{:S(2)}) %collective-permute-start.9) | collective-permute-done | bytes 65568 | tf_op jit(solution)/shard_map/ppermute | solution.py:322
  34.0 1.2 %collective-permute-start.10 = (f32[4,16,1024]{2,1,0:T(8,128)S(1)}, f32[4,16,1024]{2,1,0:T(8,128)S(1)}, u32[]{:S(2)}, u32[]{:S(2)}) collective-permute-start(f32[4,16,1024]{2,1,0:T(8,128)S(1)} %pad_maximum_fusion.2.refs_0_), channel_id=1, source_target_pairs={{0,2},{1,3},{2,0},{3,1},{4,6},{5,7},{6,4},{7,5},{8,10},{9,11},{10,... | collective-permute-start | bytes 786440 | tf_op jit(solution)/shard_map/ppermute | solution.py:319
  35.2 0.1 collective-permute-start.4
  35.3 5.5 %collective-permute-done.10.refs_1_ = f32[4,16,1024]{2,1,0:T(8,128)S(1)} collective-permute-done((f32[4,16,1024]{2,1,0:T(8,128)S(1)}, f32[4,16,1024]{2,1,0:T(8,128)S(1)}, u32[]{:S(2)}, u32[]{:S(2)}) %collective-permute-start.10) | collective-permute-done | bytes 262176 | tf_op jit(solution)/shard_map/ppermute | solution.py:319
  40.8 0.1 collective-permute-start.11
  40.9 0.7 %collective-permute-start.5 = (f32[2,16,1024]{2,1,0:T(8,128)S(1)}, f32[2,16,1024]{2,1,0:T(8,128)S(1)}, u32[]{:S(2)}, u32[]{:S(2)}) collective-permute-start(f32[2,16,1024]{2,1,0:T(8,128)S(1)} %pad_maximum_fusion.6), channel_id=1, source_target_pairs={{0,16},{4,20},{8,24},{12,28},{16,0},{20,4},{24,8},{28,12},{1,17},{... | collective-permute-start | bytes 393224 | tf_op jit(solution)/shard_map/ppermute | solution.py:322
  41.7 0.0 copy-start.5
  41.7 0.0 collective-permute-done.16.refs_2_
  41.7 2.9 %collective-permute-start.6 = (f32[2,16,1024]{2,1,0:T(8,128)S(1)}, f32[2,16,1024]{2,1,0:T(8,128)S(1)}, u32[]{:S(2)}, u32[]{:S(2)}) collective-permute-start(f32[2,16,1024]{2,1,0:T(8,128)S(1)} %pad_maximum_fusion.7), channel_id=1, source_target_pairs={{0,24},{4,28},{8,16},{12,20},{16,8},{20,12},{24,0},{28,4},{1,25},{... | collective-permute-start | bytes 393224 | tf_op jit(solution)/shard_map/ppermute | solution.py:322
  44.5 0.0 collective-permute-done.17.refs_3_
  44.5 1.8 %shard_map.73.refs_3_ = f32[42,8192]{1,0:T(8,128)} custom-call(f32[64,168]{1,0:T(8,128)S(1)} %bitcast.20, f32[4,16,1024]{2,1,0:T(8,128)S(1)} %pad_maximum_fusion.3.refs_0_, f32[4,16,1024]{2,1,0:T(8,128)S(1)} %collective-permute-done.15.refs_1_, f32[4,16,1024]{2,1,0:T(8,128)S(1)} %collective-permute-done.16.refs_2_, ...), custom_call_target="tpu_custom_call" | custom-call | flops 2000000000 | tf_op jit(solution)/shard_map/pallas_call | solution.py:418
  46.3 0.0 collective-permute-done.4.refs_1_
  46.4 7.5 %collective-permute-done.5.refs_2_ = f32[2,16,1024]{2,1,0:T(8,128)S(1)} collective-permute-done((f32[2,16,1024]{2,1,0:T(8,128)S(1)}, f32[2,16,1024]{2,1,0:T(8,128)S(1)}, u32[]{:S(2)}, u32[]{:S(2)}) %collective-permute-start.5) | collective-permute-done | bytes 131104 | tf_op jit(solution)/shard_map/ppermute | solution.py:322
  53.9 0.0 collective-permute-done.6.refs_3_
  53.9 0.0 copy-done.5
  53.9 1.6 %shard_map.72.increment_ref = f32[3,16,4096]{2,1,0:T(8,128)S(1)} custom-call(s32[8,128]{1,0:T(8,128)S(1)} %get-tuple-element.18.table_ref, s32[32,128]{1,0:T(8,128)S(1)} %get-tuple-element.19.rank_ref, s32[32,128]{1,0:T(8,128)S(1)} %bitcast.23, f32[3,16,4096]{2,1,0:T(8,128)S(1)} %get-tuple-element.21.slope_ref, ...), custom_call_target="tpu_custom_call" | custom-call | flops 1000000000 | tf_op jit(solution)/shard_map/pallas_call | solution.py:428
  55.5 0.0 collective-permute-done.11.refs_2_
  55.5 1.8 %shard_map.74 = (f32[42,8192]{1,0:T(8,128)}, f32[3,16,4096]{2,1,0:T(8,128)}) custom-call(f32[3,16,4096]{2,1,0:T(8,128)S(1)} %shard_map.72.increment_ref, f32[64,168]{1,0:T(8,128)S(1)} %bitcast.21, f32[4,16,1024]{2,1,0:T(8,128)S(1)} %pad_maximum_fusion.2.refs_0_, f32[4,16,1024]{2,1,0:T(8,128)S(1)} %collective-permute-done.10.refs_1_, ...), custom_call_target="tpu_custom_call", output_to_operand_aliasing={{0}: (5, {})} | custom-call | flops 2000000000 | tf_op jit(solution)/shard_map/pallas_call | solution.py:436
  (12 shorter events, 0.3 us)
Async XLA Ops:
  0.6 3.8 %collective-permute-start = (f32[42,8192]{1,0:T(8,128)}, f32[42,8192]{1,0:T(8,128)S(1)}, u32[]{:S(2)}, u32[]{:S(2)}) collective-permute-start(f32[42,8192]{1,0:T(8,128)} %own_ref.3), channel_id=1, source_target_pairs={{0,1},{1,0},{2,3},{3,2},{4,5},{5,4},{6,7},{7,6},{8,9},{9,8},{10,11... | collective-permute-start | bytes 4128776 | tf_op jit(solution)/shard_map/ppermute | solution.py:319
  1.2 0.7 %copy-start.4 = (s32[4096,1]{0,1:T(1,128)S(1)}, s32[4096,1]{0,1:T(1,128)}, u32[]{:S(2)}) copy-start(s32[4096,1]{0,1:T(1,128)} %param.7) | copy-start | bytes 49156
  1.9 2.5 %copy-start = (f32[42,8192]{1,0:T(8,128)S(1)}, f32[42,8192]{1,0:T(8,128)}, u32[]{:S(2)}) copy-start(f32[42,8192]{1,0:T(8,128)} %own_ref.3) | copy-start | bytes 4128772
  1.9 2.5 %copy-start.3 = (f32[1,168,64]{1,2,0:T(8,128)S(1)}, f32[1,168,64]{1,2,0:T(8,128)}, u32[]{:S(2)}) copy-start(f32[1,168,64]{1,2,0:T(8,128)} %param.8) | copy-start | bytes 129028
  4.4 4.1 %copy-start.1 = (f32[3,16,4096]{2,1,0:T(8,128)S(1)}, f32[3,16,4096]{2,1,0:T(8,128)}, u32[]{:S(2)}) copy-start(f32[3,16,4096]{2,1,0:T(8,128)} %mixing_ref.1) | copy-start | bytes 2359300
  4.4 4.1 %copy-start.2 = (f32[16,4096]{1,0:T(8,128)S(1)}, f32[16,4096]{1,0:T(8,128)}, u32[]{:S(2)}) copy-start(f32[16,4096]{1,0:T(8,128)} %density_ref.1) | copy-start | bytes 786436
  5.6 12.7 %collective-permute-start.2 = (f32[4,16,1024]{2,1,0:T(8,128)S(1)}, f32[4,16,1024]{2,1,0:T(8,128)S(1)}, u32[]{:S(2)}, u32[]{:S(2)}) collective-permute-start(f32[4,16,1024]{2,1,0:T(8,128)S(1)} %get-tuple-element.25), channel_id=1, source_target_pairs={{0,2},{1,3},{2,0},{3,1},{4,6},{5,7},{6,4},{7,5},{8,10},{9,11},{10,... | collective-permute-start | bytes 786440 | tf_op jit(solution)/shard_map/ppermute | solution.py:319
  12.4 7.8 %collective-permute-start.12 = (f32[16,1024]{1,0:T(8,128)S(1)}, f32[16,1024]{1,0:T(8,128)S(1)}, u32[]{:S(2)}, u32[]{:S(2)}) collective-permute-start(f32[16,1024]{1,0:T(8,128)S(1)} %get-tuple-element.31), channel_id=1, source_target_pairs={{0,8},{4,12},{8,0},{12,4},{16,24},{20,28},{24,16},{28,20},{1,9},{5... | collective-permute-start | bytes 196616 | tf_op jit(solution)/shard_map/ppermute | solution.py:322
  14.1 7.3 %collective-permute-start.13 = (f32[16,1024]{1,0:T(8,128)S(1)}, f32[16,1024]{1,0:T(8,128)S(1)}, u32[]{:S(2)}, u32[]{:S(2)}) collective-permute-start(f32[16,1024]{1,0:T(8,128)S(1)} %get-tuple-element.32), channel_id=1, source_target_pairs={{0,16},{4,20},{8,24},{12,28},{16,0},{20,4},{24,8},{28,12},{1,17},{... | collective-permute-start | bytes 196616 | tf_op jit(solution)/shard_map/ppermute | solution.py:322
  16.6 6.1 %collective-permute-start.14 = (f32[16,1024]{1,0:T(8,128)S(1)}, f32[16,1024]{1,0:T(8,128)S(1)}, u32[]{:S(2)}, u32[]{:S(2)}) collective-permute-start(f32[16,1024]{1,0:T(8,128)S(1)} %get-tuple-element.33), channel_id=1, source_target_pairs={{0,24},{4,28},{8,16},{12,20},{16,8},{20,12},{24,0},{28,4},{1,25},{... | collective-permute-start | bytes 196616 | tf_op jit(solution)/shard_map/ppermute | solution.py:322
  17.9 9.0 %collective-permute-start.1 = (f32[4,16,1024]{2,1,0:T(8,128)S(1)}, f32[4,16,1024]{2,1,0:T(8,128)S(1)}, u32[]{:S(2)}, u32[]{:S(2)}) collective-permute-start(f32[4,16,1024]{2,1,0:T(8,128)S(1)} %get-tuple-element.23), channel_id=1, source_target_pairs={{0,2},{1,3},{2,0},{3,1},{4,6},{5,7},{6,4},{7,5},{8,10},{9,11},{10,... | collective-permute-start | bytes 786440 | tf_op jit(solution)/shard_map/ppermute | solution.py:319
  18.4 13.5 %collective-permute-start.3 = (f32[5,16,1024]{2,1,0:T(8,128)S(1)}, f32[5,16,1024]{2,1,0:T(8,128)S(1)}, u32[]{:S(2)}, u32[]{:S(2)}) collective-permute-start(f32[5,16,1024]{2,1,0:T(8,128)S(1)} %pad_maximum_fusion.1), channel_id=1, source_target_pairs={{0,4},{4,0},{8,12},{12,8},{16,20},{20,16},{24,28},{28,24},{1,5},{5... | collective-permute-start | bytes 983048 | tf_op jit(solution)/shard_map/ppermute | solution.py:322
  22.8 9.0 %collective-permute-start.15 = (f32[4,16,1024]{2,1,0:T(8,128)S(1)}, f32[4,16,1024]{2,1,0:T(8,128)S(1)}, u32[]{:S(2)}, u32[]{:S(2)}) collective-permute-start(f32[4,16,1024]{2,1,0:T(8,128)S(1)} %pad_maximum_fusion.3.refs_0_), channel_id=1, source_target_pairs={{0,2},{1,3},{2,0},{3,1},{4,6},{5,7},{6,4},{7,5},{8,10},{9,11},{10,... | collective-permute-start | bytes 786440 | tf_op jit(solution)/shard_map/ppermute | solution.py:319
  23.3 9.1 %collective-permute-start.7 = (f32[16,1024]{1,0:T(8,128)S(1)}, f32[16,1024]{1,0:T(8,128)S(1)}, u32[]{:S(2)}, u32[]{:S(2)}) collective-permute-start(f32[16,1024]{1,0:T(8,128)S(1)} %get-tuple-element.27), channel_id=1, source_target_pairs={{0,12},{4,8},{8,4},{12,0},{16,28},{20,24},{24,20},{28,16},{1,13},{... | collective-permute-start | bytes 196616 | tf_op jit(solution)/shard_map/ppermute | solution.py:322
  24.1 8.3 %collective-permute-start.8 = (f32[16,1024]{1,0:T(8,128)S(1)}, f32[16,1024]{1,0:T(8,128)S(1)}, u32[]{:S(2)}, u32[]{:S(2)}) collective-permute-start(f32[16,1024]{1,0:T(8,128)S(1)} %get-tuple-element.28), channel_id=1, source_target_pairs={{0,20},{4,16},{8,28},{12,24},{16,4},{20,0},{24,12},{28,8},{1,21},{... | collective-permute-start | bytes 196616 | tf_op jit(solution)/shard_map/ppermute | solution.py:322
  27.0 7.0 %collective-permute-start.9 = (f32[16,1024]{1,0:T(8,128)S(1)}, f32[16,1024]{1,0:T(8,128)S(1)}, u32[]{:S(2)}, u32[]{:S(2)}) collective-permute-start(f32[16,1024]{1,0:T(8,128)S(1)} %get-tuple-element.29), channel_id=1, source_target_pairs={{0,28},{4,24},{8,20},{12,16},{16,12},{20,8},{24,4},{28,0},{1,29},{... | collective-permute-start | bytes 196616 | tf_op jit(solution)/shard_map/ppermute | solution.py:322
  31.8 9.9 %collective-permute-start.16 = (f32[4,16,1024]{2,1,0:T(8,128)S(1)}, f32[4,16,1024]{2,1,0:T(8,128)S(1)}, u32[]{:S(2)}, u32[]{:S(2)}) collective-permute-start(f32[4,16,1024]{2,1,0:T(8,128)S(1)} %pad_maximum_fusion.3.refs_0_), channel_id=1, source_target_pairs={{0,1},{1,0},{2,3},{3,2},{4,5},{5,4},{6,7},{7,6},{8,9},{9,8},{10,11... | collective-permute-start | bytes 786440 | tf_op jit(solution)/shard_map/ppermute | solution.py:319
  31.9 12.7 %collective-permute-start.17 = (f32[4,16,1024]{2,1,0:T(8,128)S(1)}, f32[4,16,1024]{2,1,0:T(8,128)S(1)}, u32[]{:S(2)}, u32[]{:S(2)}) collective-permute-start(f32[4,16,1024]{2,1,0:T(8,128)S(1)} %collective-permute-done.15.refs_1_), channel_id=1, source_target_pairs={{0,1},{1,0},{2,3},{3,2},{4,5},{5,4},{6,7},{7,6},{8,9},{9,8},{10,11... | collective-permute-start | bytes 786440 | tf_op jit(solution)/shard_map/ppermute | solution.py:319
  34.0 6.8 %collective-permute-start.10 = (f32[4,16,1024]{2,1,0:T(8,128)S(1)}, f32[4,16,1024]{2,1,0:T(8,128)S(1)}, u32[]{:S(2)}, u32[]{:S(2)}) collective-permute-start(f32[4,16,1024]{2,1,0:T(8,128)S(1)} %pad_maximum_fusion.2.refs_0_), channel_id=1, source_target_pairs={{0,2},{1,3},{2,0},{3,1},{4,6},{5,7},{6,4},{7,5},{8,10},{9,11},{10,... | collective-permute-start | bytes 786440 | tf_op jit(solution)/shard_map/ppermute | solution.py:319
  35.2 11.2 %collective-permute-start.4 = (f32[2,16,1024]{2,1,0:T(8,128)S(1)}, f32[2,16,1024]{2,1,0:T(8,128)S(1)}, u32[]{:S(2)}, u32[]{:S(2)}) collective-permute-start(f32[2,16,1024]{2,1,0:T(8,128)S(1)} %pad_maximum_fusion.5), channel_id=1, source_target_pairs={{0,8},{4,12},{8,0},{12,4},{16,24},{20,28},{24,16},{28,20},{1,9},{5... | collective-permute-start | bytes 393224 | tf_op jit(solution)/shard_map/ppermute | solution.py:322
  40.8 14.6 %collective-permute-start.11 = (f32[2,4,16,1024]{3,2,1,0:T(8,128)S(1)}, f32[2,4,16,1024]{3,2,1,0:T(8,128)S(1)}, u32[]{:S(2)}, u32[]{:S(2)}) collective-permute-start(f32[2,4,16,1024]{3,2,1,0:T(8,128)S(1)} %pad_maximum_fusion), channel_id=1, source_target_pairs={{0,1},{1,0},{2,3},{3,2},{4,5},{5,4},{6,7},{7,6},{8,9},{9,8},{10,11... | collective-permute-start | bytes 1572872 | tf_op jit(solution)/shard_map/ppermute | solution.py:319
  40.9 13.0 %collective-permute-start.5 = (f32[2,16,1024]{2,1,0:T(8,128)S(1)}, f32[2,16,1024]{2,1,0:T(8,128)S(1)}, u32[]{:S(2)}, u32[]{:S(2)}) collective-permute-start(f32[2,16,1024]{2,1,0:T(8,128)S(1)} %pad_maximum_fusion.6), channel_id=1, source_target_pairs={{0,16},{4,20},{8,24},{12,28},{16,0},{20,4},{24,8},{28,12},{1,17},{... | collective-permute-start | bytes 393224 | tf_op jit(solution)/shard_map/ppermute | solution.py:322
  41.7 12.2 %copy-start.5 = (s32[4096,1]{0,1:T(1,128)S(1)}, s32[4096,1]{0,1:T(1,128)}, u32[]{:S(2)}) copy-start(s32[4096,1]{0,1:T(1,128)} %param.7) | copy-start | bytes 49156
  41.7 12.2 %collective-permute-start.6 = (f32[2,16,1024]{2,1,0:T(8,128)S(1)}, f32[2,16,1024]{2,1,0:T(8,128)S(1)}, u32[]{:S(2)}, u32[]{:S(2)}) collective-permute-start(f32[2,16,1024]{2,1,0:T(8,128)S(1)} %pad_maximum_fusion.7), channel_id=1, source_target_pairs={{0,24},{4,28},{8,16},{12,20},{16,8},{20,12},{24,0},{28,4},{1,25},{... | collective-permute-start | bytes 393224 | tf_op jit(solution)/shard_map/ppermute | solution.py:322

commit v3 on v2

--- a/solution.py
+++ b/solution.py
@@ -199,7 +199,7 @@
             out_ref[s] = total[i * levels:(i + 1) * levels]
         return carry
 
-    lax.fori_loop(0, len(group), step, 0)
+    lax.fori_loop(0, len(group), step, 0, unroll=2)
 
 
 def gate_part(targets, group, w_ref, sources, out_any, buffer, picked_ref, sem):
@@ -208,28 +208,23 @@
     order = [mine ^ (2 * (i % half)) ^ (i // half) for i in range(len(sources))]
     pick_weights(w_ref, picked_ref, order, mine)
     capacity = sources[0].shape[-1]
-    me = first_target(targets)
     weights = picked_ref[...].T
-
-    def column(s):
-        return pl.ds(pl.multiple_of(((group.start + group.step * s) ^ me) * capacity, capacity), capacity)
-
-    def store(s):
-        part = pl.ds(pl.multiple_of(s * capacity, capacity), capacity)
-        return pltpu.make_async_copy(buffer.at[:, part], out_any.at[:, column(s)], sem.at[s])
 
     def step(s, carry):
         part = pl.ds(pl.multiple_of(s * capacity, capacity), capacity)
         buffer[:, part] = split_dot(weights, jnp.concatenate([ref[s] for ref in sources], 0))
-        store(s).start()
+        if out_any is not None:
+            gate_store(targets, group, capacity, out_any, buffer, sem, s).start()
         return carry
 
-    def finish(s, carry):
-        store(s).wait()
-        return carry
-
-    lax.fori_loop(0, len(group), step, 0)
-    return lambda: lax.fori_loop(0, len(group), finish, 0)
+    lax.fori_loop(0, len(group), step, 0, unroll=2)
+
+
+def gate_store(targets, group, capacity, out_any, buffer, sem, s):
+    at = (group.start + group.step * s) ^ first_target(targets)
+    column = pl.ds(pl.multiple_of(at * capacity, capacity), capacity)
+    part = pl.ds(pl.multiple_of(s * capacity, capacity), capacity)
+    return pltpu.make_async_copy(buffer.at[:, part], out_any.at[:, column], sem.at[s])
 
 
 def increment_kernel(targets, table_ref, rank_ref, t_ref, slope_ref, *refs):
@@ -280,17 +275,28 @@
 
 
 def gate_kernel(targets, group, picks, w_ref, *refs):
-    out_any, buffer, picked_ref, sem = refs[-4:]
-    sources = picked_sources(refs, picks)
-    gate_part(targets, group, w_ref, sources, out_any, buffer, picked_ref, sem)()
-
-
-def final_kernel(targets, group, picks, columns, increment_ref, w_ref, *refs):
+    buffer, picked_ref = refs[-2:]
+    gate_part(targets, group, w_ref, picked_sources(refs[:-2], picks), None, buffer, picked_ref, None)
+
+
+def final_kernel(targets, groups, picks, columns, increment_ref, w_ref, *refs):
     sources = picked_sources(refs[:columns], picks)
-    gate_any, out_any, buffer, picked_ref, gate_sem, out_sem = refs[-6:]
+    gate_any, out_any, buffer, picked_ref, out_sem, *sems = refs[columns + len(groups) - 1:]
+    buffers = [*refs[columns:columns + len(groups) - 1], buffer]
+    capacity = sources[0].shape[-1]
     store = pltpu.make_async_copy(increment_ref, out_any, out_sem)
     store.start()
-    gate_part(targets, group, w_ref, sources, gate_any, buffer, picked_ref, gate_sem)()
+    stores = [
+        [gate_store(targets, group, capacity, gate_any, held, sem, s) for s in range(len(group))]
+        for group, held, sem in zip(groups, buffers, sems)
+    ]
+    for copies in stores[:-1]:
+        for copy in copies:
+            copy.start()
+    gate_part(targets, groups[-1], w_ref, sources, gate_any, buffer, picked_ref, sems[-1])
+    for copies in stores:
+        for copy in copies:
+            copy.wait()
     store.wait()
 
 
@@ -402,28 +408,22 @@
     late = jnp.stack([arrived[-1]] + passed[-1])
     beside.append([swap(late, 1)])
 
-    gate_values = None
+    gates = []
     for n, (group, here) in enumerate(zip(sites, arrived)):
         final = n + 1 == len(sites)
         columns = [here] + passed[n] + beside[n]
         picks = [(i, None) for i in range(far)]
         picks += [(far, m) if final else (far + m, None) for m in range(far)]
-        before = [] if gate_values is None else [gate_values]
-        gate_scratch = [
-            pltpu.VMEM((gate_dev, len(group) * capacity), f32),
-            pltpu.VMEM(weights.shape[:1] + (gate_dev,), f32),
-            pltpu.SemaphoreType.DMA((len(group),)),
-        ]
+        picked = pltpu.VMEM(weights.shape[:1] + (gate_dev,), f32)
         if not final:
-            gate_values = pl.pallas_call(
+            gates.append(pl.pallas_call(
                 functools.partial(gate_kernel, tile_count, group, picks),
-                out_shape=shape(gate_adjoint.shape, f32),
-                in_specs=[full()] * (1 + len(columns)) + [full(pltpu.HBM)] * len(before),
-                out_specs=full(pltpu.HBM),
-                input_output_aliases={1 + len(columns): 0} if before else {},
-                scratch_shapes=gate_scratch,
+                out_shape=shape((gate_dev, len(group) * capacity), f32),
+                in_specs=[full()] * (1 + len(columns)),
+                out_specs=full(),
+                scratch_shapes=[picked],
                 **settings(12, 2),
-            )(weights, *columns, *before)
+            )(weights, *columns))
             continue
         found = pl.pallas_call(
             functools.partial(increment_kernel, tile_count),
@@ -432,16 +432,19 @@
             out_specs=full(),
             **settings(12, 1),
         )(table, rank, t, slopes, *restored)
-        operands = [found, weights, *columns]
+        operands = [found, weights, *columns, *gates]
         gate_values, increments = pl.pallas_call(
-            functools.partial(final_kernel, tile_count, group, picks, len(columns)),
+            functools.partial(final_kernel, tile_count, sites, picks, len(columns)),
             out_shape=[shape(gate_adjoint.shape, f32), shape(mixing.shape, f32)],
-            in_specs=[full()] * len(operands) + [full(pltpu.HBM)] * len(before),
+            in_specs=[full()] * len(operands),
             out_specs=[full(pltpu.HBM)] * 2,
-            input_output_aliases={len(operands): 0} if before else {},
-            scratch_shapes=gate_scratch + [pltpu.SemaphoreType.DMA],
+            scratch_shapes=[
+                pltpu.VMEM((gate_dev, len(group) * capacity), f32),
+                picked,
+                pltpu.SemaphoreType.DMA,
+            ] + [pltpu.SemaphoreType.DMA((len(site),)) for site in sites],
             **settings(16, 2),
-        )(*operands, *before)
+        )(*operands)
     return gate_values, increments
 
 

time: 57.5 us -> 56.7 us (0.986)
  Pallas kernels: 11.5 us -> 9.62 us
  waiting for transfers between devices: 19.5 us -> 20.4 us
    ppermute x10, waiting for transfers between devices: 11.7 us -> 13.1 us  [exchange(): return lax.ppermute(x, 'tile', [(i, i ^ bits) for i in range(tile_count)])]
    pallas_call x1, Pallas kernels: 1.77 us -> 0.73 us  [per_device(): pl.pallas_call(functools.partial(gate_kernel, tile_count, group, picks),...]
    pallas_call x2, Pallas kernels: 2.18 us -> 1.58 us  [per_device(): pl.pallas_call(functools.partial(adjoint_kernel, tile_count, group), out_...]
  transfers between devices with their start and end apart: 18 -> 18, of which waited for: 7 -> 6; matrix products, arithmetic and copies ran while one was open for 0% -> 0% of each run, Pallas kernels for 15% -> 13%
where the time goes in v3:
time: 56.7 us; the launch traced here: 56.4 us
  starting transfers between devices  24.5 us (43%)
  waiting for transfers between devices  20.4 us (36%)
  Pallas kernels  9.62 us (17%)
  between operations  0.82 us (1%)
  local copies, waits for them, and re-layouts  0.78 us (1%)
    ppermute x10, starting transfers between devices, exchange(): return lax.ppermute(x, 'tile', [(i, i ^ bits) for i in range(tile_count)])  17.9 us
    ppermute x10, waiting for transfers between devices, exchange(): return lax.ppermute(x, 'tile', [(i, i ^ bits) for i in range(tile_count)])  13.1 us
    ppermute x8, waiting for transfers between devices, swap(): return lax.ppermute(x, 'lev', [(i, i ^ bits) for i in range(level_count)])  7.36 us
    ppermute x8, starting transfers between devices, swap(): return lax.ppermute(x, 'lev', [(i, i ^ bits) for i in range(level_count)])  6.6 us
    pallas_call x1, Pallas kernels, per_device(): pl.pallas_call(functools.partial(source_kernel, tile_count), out_shape=[s...  3.82 us
    pallas_call x2, Pallas kernels, per_device(): pl.pallas_call(functools.partial(adjoint_kernel, tile_count, group), out_...  1.58 us
    pallas_call x1, Pallas kernels, per_device(): pl.pallas_call(functools.partial(increment_kernel, tile_count), out_shape...  1.56 us
    pallas_call x1, Pallas kernels, per_device(): pl.pallas_call(functools.partial(final_kernel, tile_count, sites, picks,...  1.53 us
  transfers between devices with their start and end apart: 18, of which 6 were waited for; matrix products, arithmetic and copies ran while one was open for 0% of the time, Pallas kernels for 13%

profile of v3, /device:TPU:0, one launch (start us, length us, event | category | flops | bytes accessed | tf_op | source)
XLA Modules:
  0.0 56.4 jit_solution(14946556477701017631)
XLA Ops:
  0.6 0.6 collective-permute-start
  1.2 0.0 copy-start.4
  1.2 0.7 %copy-done.4 = s32[4096,1]{0,1:T(1,128)S(1)} copy-done((s32[4096,1]{0,1:T(1,128)S(1)}, s32[4096,1]{0,1:T(1,128)}, u32[]{:S(2)}) %copy-start.4) | copy-done | bytes 16408
  1.9 0.0 copy-start
  1.9 0.0 copy-start.3
  1.9 0.4 shard_map.68
  2.3 2.1 %collective-permute-done.near_ref = f32[42,8192]{1,0:T(8,128)S(1)} collective-permute-done((f32[42,8192]{1,0:T(8,128)}, f32[42,8192]{1,0:T(8,128)S(1)}, u32[]{:S(2)}, u32[]{:S(2)}) %collective-permute-start) | collective-permute-done | bytes 1376288 | tf_op jit(solution)/shard_map/ppermute | solution.py:325
  4.4 0.0 copy-done
  4.4 0.0 copy-done.3
  4.4 0.0 copy-start.1
  4.4 0.0 copy-start.2
  4.4 0.8 %shard_map.71 = (f32[4,16,1024]{2,1,0:T(8,128)S(1)}, f32[4,16,1024]{2,1,0:T(8,128)S(1)}) custom-call(f32[64,168]{1,0:T(8,128)S(1)} %bitcast.18, f32[42,8192]{1,0:T(8,128)S(1)} %copy-done, f32[42,8192]{1,0:T(8,128)S(1)} %collective-permute-done.near_ref), custom_call_target="tpu_custom_call" | custom-call | flops 2000000000 | tf_op jit(solution)/shard_map/pallas_call | solution.py:365
  5.3 3.0 %collective-permute-start.2 = (f32[4,16,1024]{2,1,0:T(8,128)S(1)}, f32[4,16,1024]{2,1,0:T(8,128)S(1)}, u32[]{:S(2)}, u32[]{:S(2)}) collective-permute-start(f32[4,16,1024]{2,1,0:T(8,128)S(1)} %get-tuple-element.25), channel_id=1, source_target_pairs={{0,2},{1,3},{2,0},{3,1},{4,6},{5,7},{6,4},{7,5},{8,10},{9,11},{10,... | collective-permute-start | bytes 786440 | tf_op jit(solution)/shard_map/ppermute | solution.py:325
  8.3 0.0 copy-done.1
  8.3 0.0 copy-done.2
  8.3 3.8 %shard_map.69 = (f32[3,16,4096]{2,1,0:T(8,128)S(1)}, f32[16,1024]{1,0:T(8,128)S(1)}, f32[16,1024]{1,0:T(8,128)S(1)}, f32[16,1024]{1,0:T(8,128)S(1)}, f32[16,1024...) custom-call(s32[8,128]{1,0:T(8,128)S(1)} %get-tuple-element.18.table, ...), custom_call_target="tpu_custom_call" | custom-call | flops 4000000000 | tf_op jit(solution)/shard_map/pallas_call | solution.py:350
  12.1 1.6 %collective-permute-start.12 = (f32[16,1024]{1,0:T(8,128)S(1)}, f32[16,1024]{1,0:T(8,128)S(1)}, u32[]{:S(2)}, u32[]{:S(2)}) collective-permute-start(f32[16,1024]{1,0:T(8,128)S(1)} %get-tuple-element.31), channel_id=1, source_target_pairs={{0,8},{4,12},{8,0},{12,4},{16,24},{20,28},{24,16},{28,20},{1,9},{5... | collective-permute-start | bytes 196616 | tf_op jit(solution)/shard_map/ppermute | solution.py:328
  13.8 2.6 %collective-permute-start.13 = (f32[16,1024]{1,0:T(8,128)S(1)}, f32[16,1024]{1,0:T(8,128)S(1)}, u32[]{:S(2)}, u32[]{:S(2)}) collective-permute-start(f32[16,1024]{1,0:T(8,128)S(1)} %get-tuple-element.32), channel_id=1, source_target_pairs={{0,16},{4,20},{8,24},{12,28},{16,0},{20,4},{24,8},{28,12},{1,17},{... | collective-permute-start | bytes 196616 | tf_op jit(solution)/shard_map/ppermute | solution.py:328
  16.3 0.2 collective-permute-start.14
  16.6 0.8 %shard_map.70 = (f32[4,16,1024]{2,1,0:T(8,128)S(1)}, f32[4,16,1024]{2,1,0:T(8,128)S(1)}) custom-call(f32[64,168]{1,0:T(8,128)S(1)} %bitcast.19, f32[42,8192]{1,0:T(8,128)S(1)} %copy-done, f32[42,8192]{1,0:T(8,128)S(1)} %collective-permute-done.near_ref), custom_call_target="tpu_custom_call" | custom-call | flops 2000000000 | tf_op jit(solution)/shard_map/pallas_call | solution.py:365
  17.3 0.4 collective-permute-start.1
  17.7 0.0 collective-permute-done.2
  17.8 1.8 %collective-permute-start.3 = (f32[5,16,1024]{2,1,0:T(8,128)S(1)}, f32[5,16,1024]{2,1,0:T(8,128)S(1)}, u32[]{:S(2)}, u32[]{:S(2)}) collective-permute-start(f32[5,16,1024]{2,1,0:T(8,128)S(1)} %pad_maximum_fusion.1), channel_id=1, source_target_pairs={{0,4},{4,0},{8,12},{12,8},{16,20},{20,16},{24,28},{28,24},{1,5},{5... | collective-permute-start | bytes 983048 | tf_op jit(solution)/shard_map/ppermute | solution.py:328
  19.6 0.0 collective-permute-done.12
  19.6 1.5 %collective-permute-done.13 = f32[16,1024]{1,0:T(8,128)S(1)} collective-permute-done((f32[16,1024]{1,0:T(8,128)S(1)}, f32[16,1024]{1,0:T(8,128)S(1)}, u32[]{:S(2)}, u32[]{:S(2)}) %collective-permute-start.13) | collective-permute-done | bytes 65568 | tf_op jit(solution)/shard_map/ppermute | solution.py:328
  21.0 1.4 %collective-permute-done.14 = f32[16,1024]{1,0:T(8,128)S(1)} collective-permute-done((f32[16,1024]{1,0:T(8,128)S(1)}, f32[16,1024]{1,0:T(8,128)S(1)}, u32[]{:S(2)}, u32[]{:S(2)}) %collective-permute-start.14) | collective-permute-done | bytes 65568 | tf_op jit(solution)/shard_map/ppermute | solution.py:328
  22.5 0.6 %collective-permute-start.15 = (f32[4,16,1024]{2,1,0:T(8,128)S(1)}, f32[4,16,1024]{2,1,0:T(8,128)S(1)}, u32[]{:S(2)}, u32[]{:S(2)}) collective-permute-start(f32[4,16,1024]{2,1,0:T(8,128)S(1)} %pad_maximum_fusion.3.refs_0_), channel_id=1, source_target_pairs={{0,2},{1,3},{2,0},{3,1},{4,6},{5,7},{6,4},{7,5},{8,10},{9,11},{10,... | collective-permute-start | bytes 786440 | tf_op jit(solution)/shard_map/ppermute | solution.py:325
  23.0 1.5 %collective-permute-start.7 = (f32[16,1024]{1,0:T(8,128)S(1)}, f32[16,1024]{1,0:T(8,128)S(1)}, u32[]{:S(2)}, u32[]{:S(2)}) collective-permute-start(f32[16,1024]{1,0:T(8,128)S(1)} %get-tuple-element.27), channel_id=1, source_target_pairs={{0,12},{4,8},{8,4},{12,0},{16,28},{20,24},{24,20},{28,16},{1,13},{... | collective-permute-start | bytes 196616 | tf_op jit(solution)/shard_map/ppermute | solution.py:328
  24.6 1.7 %collective-permute-start.8 = (f32[16,1024]{1,0:T(8,128)S(1)}, f32[16,1024]{1,0:T(8,128)S(1)}, u32[]{:S(2)}, u32[]{:S(2)}) collective-permute-start(f32[16,1024]{1,0:T(8,128)S(1)} %get-tuple-element.28), channel_id=1, source_target_pairs={{0,20},{4,16},{8,28},{12,24},{16,4},{20,0},{24,12},{28,8},{1,21},{... | collective-permute-start | bytes 196616 | tf_op jit(solution)/shard_map/ppermute | solution.py:328
  26.3 0.0 collective-permute-done.1
  26.3 4.8 %collective-permute-start.9 = (f32[16,1024]{1,0:T(8,128)S(1)}, f32[16,1024]{1,0:T(8,128)S(1)}, u32[]{:S(2)}, u32[]{:S(2)}) collective-permute-start(f32[16,1024]{1,0:T(8,128)S(1)} %get-tuple-element.29), channel_id=1, source_target_pairs={{0,28},{4,24},{8,20},{12,16},{16,12},{20,8},{24,4},{28,0},{1,29},{... | collective-permute-start | bytes 196616 | tf_op jit(solution)/shard_map/ppermute | solution.py:328
  31.2 0.0 collective-permute-done.15.refs_1_
  31.2 0.1 collective-permute-start.16
  31.2 0.0 collective-permute-done.3
  31.3 0.5 collective-permute-start.17
  31.8 0.0 collective-permute-done.7
  31.8 0.0 collective-permute-done.8
  31.8 1.6 %collective-permute-done.9 = f32[16,1024]{1,0:T(8,128)S(1)} collective-permute-done((f32[16,1024]{1,0:T(8,128)S(1)}, f32[16,1024]{1,0:T(8,128)S(1)}, u32[]{:S(2)}, u32[]{:S(2)}) %collective-permute-start.9) | collective-permute-done | bytes 65568 | tf_op jit(solution)/shard_map/ppermute | solution.py:328
  33.4 1.5 %collective-permute-start.10 = (f32[4,16,1024]{2,1,0:T(8,128)S(1)}, f32[4,16,1024]{2,1,0:T(8,128)S(1)}, u32[]{:S(2)}, u32[]{:S(2)}) collective-permute-start(f32[4,16,1024]{2,1,0:T(8,128)S(1)} %pad_maximum_fusion.2.refs_0_), channel_id=1, source_target_pairs={{0,2},{1,3},{2,0},{3,1},{4,6},{5,7},{6,4},{7,5},{8,10},{9,11},{10,... | collective-permute-start | bytes 786440 | tf_op jit(solution)/shard_map/ppermute | solution.py:325
  34.9 0.1 collective-permute-start.4
  35.0 5.2 %collective-permute-done.10.refs_1_ = f32[4,16,1024]{2,1,0:T(8,128)S(1)} collective-permute-done((f32[4,16,1024]{2,1,0:T(8,128)S(1)}, f32[4,16,1024]{2,1,0:T(8,128)S(1)}, u32[]{:S(2)}, u32[]{:S(2)}) %collective-permute-start.10) | collective-permute-done | bytes 262176 | tf_op jit(solution)/shard_map/ppermute | solution.py:325
  40.2 0.1 collective-permute-start.11
  40.3 0.7 %collective-permute-start.5 = (f32[2,16,1024]{2,1,0:T(8,128)S(1)}, f32[2,16,1024]{2,1,0:T(8,128)S(1)}, u32[]{:S(2)}, u32[]{:S(2)}) collective-permute-start(f32[2,16,1024]{2,1,0:T(8,128)S(1)} %pad_maximum_fusion.6), channel_id=1, source_target_pairs={{0,16},{4,20},{8,24},{12,28},{16,0},{20,4},{24,8},{28,12},{1,17},{... | collective-permute-start | bytes 393224 | tf_op jit(solution)/shard_map/ppermute | solution.py:328
  41.1 0.0 copy-start.5
  41.1 0.0 collective-permute-done.16.refs_2_
  41.1 2.9 %collective-permute-start.6 = (f32[2,16,1024]{2,1,0:T(8,128)S(1)}, f32[2,16,1024]{2,1,0:T(8,128)S(1)}, u32[]{:S(2)}, u32[]{:S(2)}) collective-permute-start(f32[2,16,1024]{2,1,0:T(8,128)S(1)} %pad_maximum_fusion.7), channel_id=1, source_target_pairs={{0,24},{4,28},{8,16},{12,20},{16,8},{20,12},{24,0},{28,4},{1,25},{... | collective-permute-start | bytes 393224 | tf_op jit(solution)/shard_map/ppermute | solution.py:328
  43.9 0.0 collective-permute-done.17.refs_3_
  43.9 0.7 %shard_map.73.refs_3_ = f32[42,4096]{1,0:T(8,128)S(1)} custom-call(f32[64,168]{1,0:T(8,128)S(1)} %bitcast.20, f32[4,16,1024]{2,1,0:T(8,128)S(1)} %pad_maximum_fusion.3.refs_0_, f32[4,16,1024]{2,1,0:T(8,128)S(1)} %collective-permute-done.15.refs_1_, f32[4,16,1024]{2,1,0:T(8,128)S(1)} %collective-permute-done.16.refs_2_, ...), custom_call_target="tpu_custom_call" | custom-call | flops 2000000000 | tf_op jit(solution)/shard_map/pallas_call | solution.py:419
  44.7 0.0 collective-permute-done.4.refs_1_
  44.7 8.6 %collective-permute-done.5.refs_2_ = f32[2,16,1024]{2,1,0:T(8,128)S(1)} collective-permute-done((f32[2,16,1024]{2,1,0:T(8,128)S(1)}, f32[2,16,1024]{2,1,0:T(8,128)S(1)}, u32[]{:S(2)}, u32[]{:S(2)}) %collective-permute-start.5) | collective-permute-done | bytes 131104 | tf_op jit(solution)/shard_map/ppermute | solution.py:328
  53.3 0.0 collective-permute-done.6.refs_3_
  53.3 0.0 copy-done.5
  53.3 1.6 %shard_map.72.increment_ref = f32[3,16,4096]{2,1,0:T(8,128)S(1)} custom-call(s32[8,128]{1,0:T(8,128)S(1)} %get-tuple-element.18.table_ref, s32[32,128]{1,0:T(8,128)S(1)} %get-tuple-element.19.rank_ref, s32[32,128]{1,0:T(8,128)S(1)} %bitcast.23, f32[3,16,4096]{2,1,0:T(8,128)S(1)} %get-tuple-element.21.slope_ref, ...), custom_call_target="tpu_custom_call" | custom-call | flops 1000000000 | tf_op jit(solution)/shard_map/pallas_call | solution.py:428
  54.9 0.0 collective-permute-done.11.refs_2_
  54.9 1.5 %shard_map.74 = (f32[42,8192]{1,0:T(8,128)}, f32[3,16,4096]{2,1,0:T(8,128)}) custom-call(f32[3,16,4096]{2,1,0:T(8,128)S(1)} %shard_map.72.increment_ref, f32[64,168]{1,0:T(8,128)S(1)} %bitcast.21, f32[4,16,1024]{2,1,0:T(8,128)S(1)} %pad_maximum_fusion.2.refs_0_, f32[4,16,1024]{2,1,0:T(8,128)S(1)} %collective-permute-done.10.refs_1_, ...), custom_call_target="tpu_custom_call" | custom-call | flops 2000000000 | tf_op jit(solution)/shard_map/pallas_call | solution.py:436
  (12 shorter events, 0.3 us)
Async XLA Ops:
  0.6 3.8 %collective-permute-start = (f32[42,8192]{1,0:T(8,128)}, f32[42,8192]{1,0:T(8,128)S(1)}, u32[]{:S(2)}, u32[]{:S(2)}) collective-permute-start(f32[42,8192]{1,0:T(8,128)} %own_ref.3), channel_id=1, source_target_pairs={{0,1},{1,0},{2,3},{3,2},{4,5},{5,4},{6,7},{7,6},{8,9},{9,8},{10,11... | collective-permute-start | bytes 4128776 | tf_op jit(solution)/shard_map/ppermute | solution.py:325
  1.2 0.7 %copy-start.4 = (s32[4096,1]{0,1:T(1,128)S(1)}, s32[4096,1]{0,1:T(1,128)}, u32[]{:S(2)}) copy-start(s32[4096,1]{0,1:T(1,128)} %param.7) | copy-start | bytes 49156
  1.9 2.5 %copy-start = (f32[42,8192]{1,0:T(8,128)S(1)}, f32[42,8192]{1,0:T(8,128)}, u32[]{:S(2)}) copy-start(f32[42,8192]{1,0:T(8,128)} %own_ref.3) | copy-start | bytes 4128772
  1.9 2.5 %copy-start.3 = (f32[1,168,64]{1,2,0:T(8,128)S(1)}, f32[1,168,64]{1,2,0:T(8,128)}, u32[]{:S(2)}) copy-start(f32[1,168,64]{1,2,0:T(8,128)} %param.8) | copy-start | bytes 129028
  4.4 3.8 %copy-start.1 = (f32[3,16,4096]{2,1,0:T(8,128)S(1)}, f32[3,16,4096]{2,1,0:T(8,128)}, u32[]{:S(2)}) copy-start(f32[3,16,4096]{2,1,0:T(8,128)} %mixing_ref.1) | copy-start | bytes 2359300
  4.4 3.8 %copy-start.2 = (f32[16,4096]{1,0:T(8,128)S(1)}, f32[16,4096]{1,0:T(8,128)}, u32[]{:S(2)}) copy-start(f32[16,4096]{1,0:T(8,128)} %density_ref.1) | copy-start | bytes 786436
  5.3 12.5 %collective-permute-start.2 = (f32[4,16,1024]{2,1,0:T(8,128)S(1)}, f32[4,16,1024]{2,1,0:T(8,128)S(1)}, u32[]{:S(2)}, u32[]{:S(2)}) collective-permute-start(f32[4,16,1024]{2,1,0:T(8,128)S(1)} %get-tuple-element.25), channel_id=1, source_target_pairs={{0,2},{1,3},{2,0},{3,1},{4,6},{5,7},{6,4},{7,5},{8,10},{9,11},{10,... | collective-permute-start | bytes 786440 | tf_op jit(solution)/shard_map/ppermute | solution.py:325
  12.1 7.5 %collective-permute-start.12 = (f32[16,1024]{1,0:T(8,128)S(1)}, f32[16,1024]{1,0:T(8,128)S(1)}, u32[]{:S(2)}, u32[]{:S(2)}) collective-permute-start(f32[16,1024]{1,0:T(8,128)S(1)} %get-tuple-element.31), channel_id=1, source_target_pairs={{0,8},{4,12},{8,0},{12,4},{16,24},{20,28},{24,16},{28,20},{1,9},{5... | collective-permute-start | bytes 196616 | tf_op jit(solution)/shard_map/ppermute | solution.py:328
  13.8 7.3 %collective-permute-start.13 = (f32[16,1024]{1,0:T(8,128)S(1)}, f32[16,1024]{1,0:T(8,128)S(1)}, u32[]{:S(2)}, u32[]{:S(2)}) collective-permute-start(f32[16,1024]{1,0:T(8,128)S(1)} %get-tuple-element.32), channel_id=1, source_target_pairs={{0,16},{4,20},{8,24},{12,28},{16,0},{20,4},{24,8},{28,12},{1,17},{... | collective-permute-start | bytes 196616 | tf_op jit(solution)/shard_map/ppermute | solution.py:328
  16.3 6.1 %collective-permute-start.14 = (f32[16,1024]{1,0:T(8,128)S(1)}, f32[16,1024]{1,0:T(8,128)S(1)}, u32[]{:S(2)}, u32[]{:S(2)}) collective-permute-start(f32[16,1024]{1,0:T(8,128)S(1)} %get-tuple-element.33), channel_id=1, source_target_pairs={{0,24},{4,28},{8,16},{12,20},{16,8},{20,12},{24,0},{28,4},{1,25},{... | collective-permute-start | bytes 196616 | tf_op jit(solution)/shard_map/ppermute | solution.py:328
  17.3 8.9 %collective-permute-start.1 = (f32[4,16,1024]{2,1,0:T(8,128)S(1)}, f32[4,16,1024]{2,1,0:T(8,128)S(1)}, u32[]{:S(2)}, u32[]{:S(2)}) collective-permute-start(f32[4,16,1024]{2,1,0:T(8,128)S(1)} %get-tuple-element.23), channel_id=1, source_target_pairs={{0,2},{1,3},{2,0},{3,1},{4,6},{5,7},{6,4},{7,5},{8,10},{9,11},{10,... | collective-permute-start | bytes 786440 | tf_op jit(solution)/shard_map/ppermute | solution.py:325
  17.8 13.5 %collective-permute-start.3 = (f32[5,16,1024]{2,1,0:T(8,128)S(1)}, f32[5,16,1024]{2,1,0:T(8,128)S(1)}, u32[]{:S(2)}, u32[]{:S(2)}) collective-permute-start(f32[5,16,1024]{2,1,0:T(8,128)S(1)} %pad_maximum_fusion.1), channel_id=1, source_target_pairs={{0,4},{4,0},{8,12},{12,8},{16,20},{20,16},{24,28},{28,24},{1,5},{5... | collective-permute-start | bytes 983048 | tf_op jit(solution)/shard_map/ppermute | solution.py:328
  22.5 8.7 %collective-permute-start.15 = (f32[4,16,1024]{2,1,0:T(8,128)S(1)}, f32[4,16,1024]{2,1,0:T(8,128)S(1)}, u32[]{:S(2)}, u32[]{:S(2)}) collective-permute-start(f32[4,16,1024]{2,1,0:T(8,128)S(1)} %pad_maximum_fusion.3.refs_0_), channel_id=1, source_target_pairs={{0,2},{1,3},{2,0},{3,1},{4,6},{5,7},{6,4},{7,5},{8,10},{9,11},{10,... | collective-permute-start | bytes 786440 | tf_op jit(solution)/shard_map/ppermute | solution.py:325
  23.0 8.7 %collective-permute-start.7 = (f32[16,1024]{1,0:T(8,128)S(1)}, f32[16,1024]{1,0:T(8,128)S(1)}, u32[]{:S(2)}, u32[]{:S(2)}) collective-permute-start(f32[16,1024]{1,0:T(8,128)S(1)} %get-tuple-element.27), channel_id=1, source_target_pairs={{0,12},{4,8},{8,4},{12,0},{16,28},{20,24},{24,20},{28,16},{1,13},{... | collective-permute-start | bytes 196616 | tf_op jit(solution)/shard_map/ppermute | solution.py:328
  24.6 7.2 %collective-permute-start.8 = (f32[16,1024]{1,0:T(8,128)S(1)}, f32[16,1024]{1,0:T(8,128)S(1)}, u32[]{:S(2)}, u32[]{:S(2)}) collective-permute-start(f32[16,1024]{1,0:T(8,128)S(1)} %get-tuple-element.28), channel_id=1, source_target_pairs={{0,20},{4,16},{8,28},{12,24},{16,4},{20,0},{24,12},{28,8},{1,21},{... | collective-permute-start | bytes 196616 | tf_op jit(solution)/shard_map/ppermute | solution.py:328
  26.3 7.1 %collective-permute-start.9 = (f32[16,1024]{1,0:T(8,128)S(1)}, f32[16,1024]{1,0:T(8,128)S(1)}, u32[]{:S(2)}, u32[]{:S(2)}) collective-permute-start(f32[16,1024]{1,0:T(8,128)S(1)} %get-tuple-element.29), channel_id=1, source_target_pairs={{0,28},{4,24},{8,20},{12,16},{16,12},{20,8},{24,4},{28,0},{1,29},{... | collective-permute-start | bytes 196616 | tf_op jit(solution)/shard_map/ppermute | solution.py:328
  31.2 9.9 %collective-permute-start.16 = (f32[4,16,1024]{2,1,0:T(8,128)S(1)}, f32[4,16,1024]{2,1,0:T(8,128)S(1)}, u32[]{:S(2)}, u32[]{:S(2)}) collective-permute-start(f32[4,16,1024]{2,1,0:T(8,128)S(1)} %pad_maximum_fusion.3.refs_0_), channel_id=1, source_target_pairs={{0,1},{1,0},{2,3},{3,2},{4,5},{5,4},{6,7},{7,6},{8,9},{9,8},{10,11... | collective-permute-start | bytes 786440 | tf_op jit(solution)/shard_map/ppermute | solution.py:325
  31.3 12.7 %collective-permute-start.17 = (f32[4,16,1024]{2,1,0:T(8,128)S(1)}, f32[4,16,1024]{2,1,0:T(8,128)S(1)}, u32[]{:S(2)}, u32[]{:S(2)}) collective-permute-start(f32[4,16,1024]{2,1,0:T(8,128)S(1)} %collective-permute-done.15.refs_1_), channel_id=1, source_target_pairs={{0,1},{1,0},{2,3},{3,2},{4,5},{5,4},{6,7},{7,6},{8,9},{9,8},{10,11... | collective-permute-start | bytes 786440 | tf_op jit(solution)/shard_map/ppermute | solution.py:325
  33.4 6.8 %collective-permute-start.10 = (f32[4,16,1024]{2,1,0:T(8,128)S(1)}, f32[4,16,1024]{2,1,0:T(8,128)S(1)}, u32[]{:S(2)}, u32[]{:S(2)}) collective-permute-start(f32[4,16,1024]{2,1,0:T(8,128)S(1)} %pad_maximum_fusion.2.refs_0_), channel_id=1, source_target_pairs={{0,2},{1,3},{2,0},{3,1},{4,6},{5,7},{6,4},{7,5},{8,10},{9,11},{10,... | collective-permute-start | bytes 786440 | tf_op jit(solution)/shard_map/ppermute | solution.py:325
  34.9 9.8 %collective-permute-start.4 = (f32[2,16,1024]{2,1,0:T(8,128)S(1)}, f32[2,16,1024]{2,1,0:T(8,128)S(1)}, u32[]{:S(2)}, u32[]{:S(2)}) collective-permute-start(f32[2,16,1024]{2,1,0:T(8,128)S(1)} %pad_maximum_fusion.5), channel_id=1, source_target_pairs={{0,8},{4,12},{8,0},{12,4},{16,24},{20,28},{24,16},{28,20},{1,9},{5... | collective-permute-start | bytes 393224 | tf_op jit(solution)/shard_map/ppermute | solution.py:328
  40.2 14.6 %collective-permute-start.11 = (f32[2,4,16,1024]{3,2,1,0:T(8,128)S(1)}, f32[2,4,16,1024]{3,2,1,0:T(8,128)S(1)}, u32[]{:S(2)}, u32[]{:S(2)}) collective-permute-start(f32[2,4,16,1024]{3,2,1,0:T(8,128)S(1)} %pad_maximum_fusion), channel_id=1, source_target_pairs={{0,1},{1,0},{2,3},{3,2},{4,5},{5,4},{6,7},{7,6},{8,9},{9,8},{10,11... | collective-permute-start | bytes 1572872 | tf_op jit(solution)/shard_map/ppermute | solution.py:325
  40.3 13.0 %collective-permute-start.5 = (f32[2,16,1024]{2,1,0:T(8,128)S(1)}, f32[2,16,1024]{2,1,0:T(8,128)S(1)}, u32[]{:S(2)}, u32[]{:S(2)}) collective-permute-start(f32[2,16,1024]{2,1,0:T(8,128)S(1)} %pad_maximum_fusion.6), channel_id=1, source_target_pairs={{0,16},{4,20},{8,24},{12,28},{16,0},{20,4},{24,8},{28,12},{1,17},{... | collective-permute-start | bytes 393224 | tf_op jit(solution)/shard_map/ppermute | solution.py:328
  41.1 12.2 %copy-start.5 = (s32[4096,1]{0,1:T(1,128)S(1)}, s32[4096,1]{0,1:T(1,128)}, u32[]{:S(2)}) copy-start(s32[4096,1]{0,1:T(1,128)} %param.7) | copy-start | bytes 49156
  41.1 12.2 %collective-permute-start.6 = (f32[2,16,1024]{2,1,0:T(8,128)S(1)}, f32[2,16,1024]{2,1,0:T(8,128)S(1)}, u32[]{:S(2)}, u32[]{:S(2)}) collective-permute-start(f32[2,16,1024]{2,1,0:T(8,128)S(1)} %pad_maximum_fusion.7), channel_id=1, source_target_pairs={{0,24},{4,28},{8,16},{12,20},{16,8},{20,12},{24,0},{28,4},{1,25},{... | collective-permute-start | bytes 393224 | tf_op jit(solution)/shard_map/ppermute | solution.py:328
